TPU v7x, 512 devices: a whole 4x8x8 slice. The times are simulated.
512 devices in a mesh: rows: 32 (over z, x), tp: 2 (over core), job: 8 (over y).
Axes of the slice: x: 4, y: 8, z: 8, core: 2. Of those that a mesh axis runs over, the one named last changes fastest.
Arguments:
- train_query: bfloat16 [16384, 2048], P(('job', 'rows'), 'tp'), parts along dimension 0, may hold values from -0.125 to 0.125
- low_query: bfloat16 [16384, 16], P(('job', 'rows')), parts along dimension 0, may hold values from -0.125 to 0.125
- high_query: bfloat16 [128, 2048], P('job', 'tp'), parts along dimension 0, may hold values from -1.5 to 1.5
- train_key: bfloat16 [16384, 512], P(('job', 'rows'), 'tp'), parts along dimension 0, may hold values from -0.125 to 0.125
- low_key: bfloat16 [16384, 16], P(('job', 'rows')), parts along dimension 0, may hold values from -0.125 to 0.125
- high_key: bfloat16 [128, 512], P('job', 'tp'), parts along dimension 0, may hold values from -1.5 to 1.5
- train_value: bfloat16 [16384, 512], P(('job', 'rows'), 'tp'), parts along dimension 0, may hold values from -0.125 to 0.125
- low_value: bfloat16 [16384, 16], P(('job', 'rows')), parts along dimension 0, may hold values from -0.125 to 0.125
- high_value: bfloat16 [128, 512], P('job', 'tp'), parts along dimension 0, may hold values from -1.5 to 1.5
- norm_train: float32 [16384], P(('job', 'rows', 'tp')), parts along dimension 0, may hold values from 0.25 to 1.75
- norm_step: float32 [16384], P(('job', 'rows', 'tp')), parts along dimension 0, may hold values from -0.3 to 0.3
Outputs:
- serve_query: bfloat16 [16384, 2048], P(('job', 'tp')), parts along dimension 0
- serve_key: bfloat16 [4096, 2048], P(('job', 'tp')), parts along dimension 0
- serve_value: bfloat16 [4096, 2048], P(('job', 'tp')), parts along dimension 0
- serve_norm: bfloat16 [16384], P('job'), parts along dimension 0
There are 8 independent parts, one for each index of `job`. A program takes and returns all parts, laid end to end along the dimension named above; each array names one. Nothing has to cross between parts.
All inputs are finite; a program needn't handle non-finite values.
Results may differ from a plain program's by a relative error of at most 0.001.
Values may be sent and summed in bfloat16 or wider, within the bound.
No kernel may reach another device: no remote copies, remote signals or barrier semaphores. Data moves between devices by JAX's collectives and lax.ppermute only.
A program may use at most 64 MiB of HBM per device.

v0:
```python
import jax
import jax.numpy as jnp
from jax import lax
from jax.sharding import PartitionSpec as P

mix_rate = 0.5


def in_one_piece(arrays, axis, dim, along):
    widths = [a.shape[along] for a in arrays]
    both = jnp.concatenate(arrays, axis=along)
    out = lax.all_gather(both, axis, axis=dim, tiled=True)
    return tuple(jnp.split(out, [sum(widths[:k]) for k in range(1, len(widths))], axis=along))


def in_order(pieces, dim):
    pieces = jnp.moveaxis(pieces, 0, dim)
    lengths = pieces.shape
    return pieces.reshape(*lengths[:dim], lengths[dim] * lengths[dim + 1], *lengths[dim + 2 :])


def from_everyone(shard, axis):
    length = lax.axis_size(axis)
    return lax.all_to_all(
        jnp.broadcast_to(shard[None], (length, *shard.shape)), axis, 0, 0, tiled=True
    )


def gathered_copies(shard, axis, dim):
    return in_order(from_everyone(shard, axis), dim)


def local(
    train_query,
    low_query,
    high_query,
    train_key,
    low_key,
    high_key,
    train_value,
    low_value,
    high_value,
    norm_train,
    norm_step,
):
    fresh_query = train_query.astype(jnp.float32) + mix_rate * jnp.dot(
        low_query, high_query, preferred_element_type=jnp.float32
    )
    fresh_key = train_key.astype(jnp.float32) + mix_rate * jnp.dot(
        low_key, high_key, preferred_element_type=jnp.float32
    )
    fresh_value = train_value.astype(jnp.float32) + mix_rate * jnp.dot(
        low_value, high_value, preferred_element_type=jnp.float32
    )
    narrow_query, narrow_key, narrow_value = (
        fresh_query.astype(jnp.bfloat16),
        fresh_key.astype(jnp.bfloat16),
        fresh_value.astype(jnp.bfloat16),
    )
    serve_query, serve_key, serve_value = in_one_piece(
        (narrow_query, narrow_key, narrow_value), "rows", 0, 1
    )
    serve_query, serve_key, serve_value = (serve_query.T, serve_key.T, serve_value.T)
    serve_norm = gathered_copies((norm_train + norm_step).astype(jnp.bfloat16), ("rows", "tp"), 0)
    return (serve_query, serve_key, serve_value, serve_norm)


def solution(mesh):
    in_specs = (
        P(("job", "rows"), "tp"),
        P(("job", "rows"), None),
        P("job", "tp"),
        P(("job", "rows"), "tp"),
        P(("job", "rows"), None),
        P("job", "tp"),
        P(("job", "rows"), "tp"),
        P(("job", "rows"), None),
        P("job", "tp"),
        P(("job", "rows", "tp")),
        P(("job", "rows", "tp")),
    )
    out_specs = (P(("job", "tp"), None), P(("job", "tp"), None), P(("job", "tp"), None), P("job"))
    return jax.shard_map(local, mesh=mesh, in_specs=in_specs, out_specs=out_specs, check_vma=False)
```

profile of v0, /device:TPU:1, one launch (start us, length us, event | category | flops | bytes accessed | tf_op | source)
XLA Modules:
  0.0 133.6 jit_solution(12054167524016155888)
XLA Ops:
  7.2 0.0 copy-start
  7.2 0.0 all-gather.2.cloned.1.call-start
  7.2 0.7 copy-done
  7.9 1.1 fusion.1
  9.1 1.0 fusion.4
  10.0 1.0 fusion.5
  11.0 0.7 pad_maximum_fusion
  11.7 0.0 all-gather.2.cloned.1.call-update
  11.7 0.7 add_convert_fusion
  12.4 24.0 %all_to_all.6 = bf16[64,1,32]{2,1,0:T(2,128)(2,1)S(1)} all-to-all(bf16[64,1,32]{2,1,0:T(2,128)(2,1)S(1)} %broadcast_in_dim.2), channel_id=1, replica_groups=mesh['rows'=32,'tp'=2,'job'=8] {'rows','tp'}, dimensions={0} | all-to-all | bytes 8192 | tf_op jit(solution)/shard_map/all_to_all | solution.py:24
  36.5 0.1 reduce
  36.6 0.7 reshape.18
  37.2 73.9 %all-gather.2.cloned.1.call-done = bf16[2048,1536]{1,0:T(8,128)(2,1)} async-done(((bf16[64,1536]{1,0:T(8,128)(2,1)}), bf16[2048,1536]{1,0:T(8,128)(2,1)}) %all-gather.2.cloned.1.call-update) | async-done | bytes 6291472 | tf_op jit(solution)/shard_map/all_gather | solution.py:12
  111.1 1.7 %slice_bitcast_fusion.1 = (bf16[256,2048]{0,1:T(8,128)(2,1)S(1)}, bf16[256,2048]{0,1:T(8,128)(2,1)S(1)}) fusion(bf16[2048,1536]{1,0:T(8,128)(2,1)} %all-gather.2.cloned.1.call-done), kind=kLoop, calls=%fused_computation.10 | loop fusion | bytes 4194304 | tf_op jit(solution)/shard_map/transpose | solution.py:63
  112.8 1.4 %copy.22 = bf16[256,2048]{1,0:T(8,128)(2,1)} copy(bf16[256,2048]{0,1:T(8,128)(2,1)S(1)} %get-tuple-element.17) | data formatting | bytes 2097152
  114.2 1.4 %copy.23 = bf16[256,2048]{1,0:T(8,128)(2,1)} copy(bf16[256,2048]{0,1:T(8,128)(2,1)S(1)} %get-tuple-element.16) | data formatting | bytes 2097152
  115.6 4.6 %slice_bitcast_fusion = bf16[1024,2048]{0,1:T(8,128)(2,1)} fusion(bf16[2048,1536]{1,0:T(8,128)(2,1)} %all-gather.2.cloned.1.call-done), kind=kLoop, calls=%fused_computation | loop fusion | bytes 8388608 | tf_op jit(solution)/shard_map/transpose | solution.py:63
  120.3 6.4 %copy.21 = bf16[1024,2048]{1,0:T(8,128)(2,1)} copy(bf16[1024,2048]{0,1:T(8,128)(2,1)} %slice_bitcast_fusion) | data formatting | bytes 8388608
  (1 shorter events, 0.0 us)
Async XLA Ops:
  7.2 0.8 copy-start
  7.2 103.9 %all-gather.2.cloned.1.call-start = ((), (), s32[]{:S(2)}) async-start(), calls=%async_computation.1 | async-start | bytes 6488064 | tf_op jit(solution)/shard_map/all_gather | solution.py:12
Sparse Core Ops, SparseCore 0:
  11.9 99.2 all-gather.1
where the time goes:
time: 134 us
  waiting for transfers between devices  73.9 us (55%)
  blocking collectives  24 us (18%)
  local copies, waits for them, and re-layouts  17 us (13%)
  between operations  14.1 us (11%)
  matrix products  3.07 us (2%)
  other arithmetic  1.47 us (1%)
    all_gather x1, waiting for transfers between devices, in_one_piece(): out = lax.all_gather(both, axis, axis=dim, tiled=True)  73.9 us
    all_to_all x1, blocking collectives, from_everyone(): lax.all_to_all(jnp.broadcast_to(shard[None], (length, *shard.shape)), axi...  24 us
    unnamed x5, local copies, waits for them, and re-layouts  9.97 us
    transpose x2, local copies, waits for them, and re-layouts, local(): serve_query, serve_key, serve_value = (serve_query.T, serve_key.T, serve_...  6.34 us
  transfers between devices with their start and end apart: 1, of which 1 were waited for; matrix products, arithmetic and copies ran while one was open for 1% of the time, Pallas kernels for 0%

commit v1 on v0

v1 whole, which is shorter than its diff:
```python
import functools

import jax
import jax.numpy as jnp
from jax import lax
from jax.experimental import pallas as pl
from jax.experimental.pallas import tpu as pltpu
from jax.sharding import Mesh, PartitionSpec as P


mix_rate = 0.5
LANES = 128
NORM_ROWS = 8
A_Q = 2
B_CUTS = (6,)


def merge_kernel(
    tq, lq, hq, tk, lk, hk, tv, lv, hv, nt, ns, *outs
):
    out_a, outs_b = outs[0], outs[1:]

    def piece(t, l, h, lo, hi):
        low_high = lax.dot_general(
            l[...], h[:, lo:hi], (((0,), (0,)), ((), ())), preferred_element_type=jnp.float32
        )
        return (t[:, lo:hi].astype(jnp.float32) + mix_rate * low_high).astype(jnp.bfloat16)

    rows = tq.shape[0]
    at = A_Q * LANES
    for k, cut in enumerate(B_CUTS):
        w = piece(tq, lq, hq, at, at + cut * LANES)
        at += cut * LANES
        for d in range(outs_b[k].shape[0]):
            for j in range(cut):
                outs_b[k][d, j * rows : (j + 1) * rows, :] = w[:, j * LANES : (j + 1) * LANES]
    norm = (nt[...] + ns[...]).astype(jnp.bfloat16)
    norm = jnp.concatenate([norm, jnp.zeros((1, LANES - norm.shape[1]), jnp.bfloat16)], axis=1)
    norm = jnp.broadcast_to(norm, (NORM_ROWS, LANES))
    for d in range(outs_b[0].shape[0]):
        outs_b[0][d, B_CUTS[0] * rows :, :] = norm
    at = 0
    for t, l, h, width in ((tk, lk, hk, tk.shape[1]), (tv, lv, hv, tv.shape[1]), (tq, lq, hq, A_Q * LANES)):
        w = piece(t, l, h, 0, width)
        out_a[:, at : at + width] = w
        at += width


def turn_kernel(steps, *refs):
    pieces, (out, held) = refs[: len(steps)], refs[len(steps) :]
    n = len(steps)
    rows, width = pieces[0].shape
    me = lax.axis_index("x")
    for step, piece in zip(steps, pieces):
        at = pl.multiple_of(lax.rem(me + (step + n), n) * rows, rows)
        held[pl.ds(at, rows), :] = piece[...]
    for j in range(width // LANES):
        out[j * LANES : (j + 1) * LANES, :] = held[:, j * LANES : (j + 1) * LANES].T


def place_b_kernel(first, cut, rows, b, *rest):
    out, held, sem = rest[-3:]
    nx, nz = b.shape[0], b.shape[1]
    wide = nx * rows
    copies = []
    for j in range(cut):
        for z in range(nz):
            block = jnp.concatenate(
                [b[x, z, j * rows : (j + 1) * rows, :] for x in range(nx)], axis=0
            )
            held[j * LANES : (j + 1) * LANES, z * wide : (z + 1) * wide] = block.T
        copy = pltpu.make_async_copy(
            held.at[pl.ds(j * LANES, LANES), :],
            out.at[pl.ds((first + j) * LANES, LANES), :],
            sem.at[j],
        )
        copy.start()
        copies.append(copy)
    for copy in copies:
        copy.wait()


def place_a_kernel(steps, nz, wide, kv, *refs):
    n = len(steps)
    blocks = refs[:n]
    out_q, out_k, out_v, sem = refs[-4:]
    me = lax.axis_index("z")
    copies = []
    for i, (step, block) in enumerate(zip(steps, blocks)):
        at = pl.ds(pl.multiple_of(lax.rem(me + (step + nz), nz) * wide, wide), wide)
        for s, (lo, hi, out) in enumerate(
            ((0, kv, out_k), (kv, 2 * kv, out_v), (2 * kv, 2 * kv + A_Q * LANES, out_q))
        ):
            copy = pltpu.make_async_copy(
                block.at[pl.ds(lo, hi - lo), :], out.at[pl.ds(0, hi - lo), at], sem.at[i, s]
            )
            copy.start()
            copies.append(copy)
    for copy in copies:
        copy.wait()


def fan_kernel(b, out):
    for d in range(out.shape[0]):
        out[d] = b[...]


VM = pl.BlockSpec(memory_space=pltpu.VMEM)
ANY = pl.BlockSpec(memory_space=pl.ANY)


def call(kernel, ins, out_specs, out_shape, scratch=(), aliases={}, n_any=0, cost=1 << 20):
    return pl.pallas_call(
        kernel,
        in_specs=[VM] * (len(ins) - n_any) + [ANY] * n_any,
        out_specs=out_specs,
        out_shape=out_shape,
        scratch_shapes=list(scratch),
        input_output_aliases=aliases,
        cost_estimate=pl.CostEstimate(flops=cost, bytes_accessed=cost, transcendentals=0),
    )(*ins)


def shift(a, axis, by):
    n = lax.axis_size(axis)
    return lax.ppermute(a, axis, [(i, (i + by) % n) for i in range(n)])


def spread(a, axis):
    return lax.all_to_all(a, axis, 0, 0, tiled=True)


def steps_of(tq, lq, hq, tk, lk, hk, tv, lv, hv, nt, ns):
    nz, nx = lax.axis_size("z"), lax.axis_size("x")
    rows, q_wide = tq.shape
    kv = tk.shape[1]
    wide = nx * rows
    a_wide = 2 * kv + A_Q * LANES
    bf = jnp.bfloat16
    b_rows = [cut * rows + (NORM_ROWS if k == 0 else 0) for k, cut in enumerate(B_CUTS)]
    out_shape = [jax.ShapeDtypeStruct((rows, a_wide), bf)] + [
        jax.ShapeDtypeStruct((nz, r, LANES), bf) for r in b_rows
    ]
    a, *bs = call(
        merge_kernel,
        (tq, lq.T, hq, tk, lk.T, hk, tv, lv.T, hv, nt[None], ns[None]),
        [VM] * len(out_shape),
        out_shape,
    )
    b1 = []
    for b in bs:
        b1.append(spread(b, "z"))
    a1 = shift(a, "x", 1)
    a2 = shift(a, "x", -1)
    a3 = shift(a, "x", 2)
    own = call(
        functools.partial(turn_kernel, (0, -1, 1, -2)),
        (a, a1, a2, a3),
        VM,
        jax.ShapeDtypeStruct((a_wide, wide), bf),
        scratch=[pltpu.VMEM((wide, a_wide), bf)],
    )
    blocks = {0: own}
    for step in range(1, nz // 2):
        blocks[-step] = shift(blocks[1 - step], "z", 1)
        blocks[step] = shift(blocks[step - 1], "z", -1)
    blocks[-(nz // 2)] = shift(blocks[1 - nz // 2], "z", 1)
    b2 = []
    for b in b1:
        wide_b = call(fan_kernel, (b,), VM, jax.ShapeDtypeStruct((nx, *b.shape), bf))
        b2.append(spread(wide_b, "x"))
    q_shape = jax.ShapeDtypeStruct((q_wide, nz * wide), bf)
    kv_shape = jax.ShapeDtypeStruct((kv, nz * wide), bf)

    def place_b(k, out_q):
        first = A_Q + sum(B_CUTS[:k])
        cut = B_CUTS[k]
        ins = (b2[k],) if out_q is None else (b2[k], out_q)
        return call(
            functools.partial(place_b_kernel, first, cut, rows),
            ins,
            ANY,
            q_shape,
            scratch=[pltpu.VMEM((cut * LANES, nz * wide), bf), pltpu.SemaphoreType.DMA((cut,))],
            aliases={} if out_q is None else {1: 0},
            n_any=len(ins) - 1,
        )

    def place_a(steps, outs):
        ins = tuple(blocks[s] for s in steps) + outs
        n = len(steps)
        return call(
            functools.partial(place_a_kernel, steps, nz, wide, kv),
            ins,
            [ANY] * 3,
            [q_shape, kv_shape, kv_shape],
            scratch=[pltpu.SemaphoreType.DMA((n, 3))],
            aliases={n + i: i for i in range(len(outs))},
            n_any=len(outs),
        )

    half = nz // 2
    early = (0, -1, 1, -2, 2)
    late = tuple(s for s in (-3, 3, -half))
    outs = place_a(early, ())
    out_q = outs[0]
    for k in range(len(B_CUTS)):
        out_q = place_b(k, out_q)
    serve_query, serve_key, serve_value = place_a(late, (out_q, outs[1], outs[2]))
    part = nt.shape[0]
    mine = b2[0][:, :, B_CUTS[0] * rows, :part]
    mine = jnp.swapaxes(mine, 0, 1).reshape(nz * nx, part)
    other = lax.ppermute(mine, "tp", [(0, 1), (1, 0)])
    first = lax.axis_index("tp") == 0
    serve_norm = jnp.concatenate(
        [jnp.where(first, mine, other), jnp.where(first, other, mine)], axis=1
    ).reshape(-1)
    return serve_query, serve_key, serve_value, serve_norm


def solution(mesh):
    rows, tp, job = mesh.devices.shape
    nx = 4
    fine = Mesh(mesh.devices.reshape(rows // nx, nx, tp, job), ("z", "x", "tp", "job"))
    r = ("job", "z", "x")
    w, low, high, vec = P(r, "tp"), P(r, None), P("job", "tp"), P(("job", "z", "x", "tp"))
    out_specs = (P(("job", "tp"), None),) * 3 + (P("job"),)
    return jax.shard_map(
        steps_of,
        mesh=fine,
        in_specs=(w, low, high) * 3 + (vec, vec),
        out_specs=out_specs,
        check_vma=False,
    )
```

time: 134 us -> 137 us (1.022)
  starting transfers between devices: 0.04 us -> 46.5 us
  waiting for transfers between devices: 73.9 us -> 38.4 us
  Pallas kernels: 0 us -> 16.1 us
  local copies, waits for them, and re-layouts: 17 us -> 1.36 us
  between operations: 14.1 us -> 0.87 us
  blocking collectives: 24 us -> 32.9 us
  matrix products: 3.07 us -> 0 us
  other arithmetic: 1.47 us -> 0.09 us
    all_gather x1 -> x0, waiting for transfers between devices: 73.9 us -> none  [in_one_piece(): out = lax.all_gather(both, axis, axis=dim, tiled=True)]
    ppermute x0 -> x11, starting transfers between devices: none -> 42.3 us  [the longest x10 31.6 us: shift(): return lax.ppermute(a, axis, [(i, (i + by) % n) for i in range(n)])]
    ppermute x0 -> x11, waiting for transfers between devices: none -> 38.4 us  [the longest x10 38.4 us: shift(): return lax.ppermute(a, axis, [(i, (i + by) % n) for i in range(n)])]
    pallas_call x0 -> x6, Pallas kernels: none -> 16.1 us  [call(): pl.pallas_call(kernel, in_specs=[VM] * (len(ins) - n_any) + [ANY] * n_any...]
    unnamed x5 -> x15, local copies, waits for them, and re-layouts: 9.97 us -> 0.66 us
    all_to_all x1, blocking collectives: 24 us -> 32.9 us  [spread(): return lax.all_to_all(a, axis, 0, 0, tiled=True)]
    transpose x2 -> x1, local copies, waits for them, and re-layouts: 6.34 us -> 0.01 us  [steps_of(): mine = jnp.swapaxes(mine, 0, 1).reshape(nz * nx, part)]
    all_to_all x0 -> x1, starting transfers between devices: none -> 4.14 us  [spread(): return lax.all_to_all(a, axis, 0, 0, tiled=True)]
  transfers between devices with their start and end apart: 1 -> 12, of which waited for: 1 -> 5; matrix products, arithmetic and copies ran while one was open for 1% -> 0% of each run, Pallas kernels for 0% -> 8%
where the time goes in v1:
time: 137 us; the launch traced here: 136 us
  starting transfers between devices  46.5 us (34%)
  waiting for transfers between devices  38.4 us (28%)
  blocking collectives  32.9 us (24%)
  Pallas kernels  16.1 us (12%)
    ppermute x10, waiting for transfers between devices, shift(): return lax.ppermute(a, axis, [(i, (i + by) % n) for i in range(n)])  38.4 us
    all_to_all x1, blocking collectives, spread(): return lax.all_to_all(a, axis, 0, 0, tiled=True)  32.9 us
    ppermute x10, starting transfers between devices, shift(): return lax.ppermute(a, axis, [(i, (i + by) % n) for i in range(n)])  31.6 us
    pallas_call x6, Pallas kernels, call(): pl.pallas_call(kernel, in_specs=[VM] * (len(ins) - n_any) + [ANY] * n_any...  16.1 us
    ppermute x1, starting transfers between devices, steps_of(): other = lax.ppermute(mine, 'tp', [(0, 1), (1, 0)])  10.7 us
    all_to_all x1, starting transfers between devices, spread(): return lax.all_to_all(a, axis, 0, 0, tiled=True)  4.14 us
  transfers between devices with their start and end apart: 12, of which 5 were waited for; matrix products, arithmetic and copies ran while one was open for 0% of the time, Pallas kernels for 8%

profile of v1, /device:TPU:1, one launch (start us, length us, event | category | flops | bytes accessed | tf_op | source)
XLA Modules:
  0.0 136.2 jit_solution(6586365025562155423)
XLA Ops:
  0.6 2.1 %shard_map.138 = (bf16[64,768]{1,0:T(8,128)(2,1)}, bf16[8,392,128]{2,1,0:T(8,128)(2,1)}) custom-call(bf16[64,1024]{1,0:T(8,128)(2,1)} %tq.1, bf16[16,64]{1,0:T(8,128)(2,1)} %bitcast.14, bf16[16,1024]{1,0:T(8,128)(2,1)} %hq.1, bf16[64,256]{1,0:T(8,128)(2,1)} %tk.1, bf16[16,64]{1,0:T(8,128)(2,1)} %bitcast.15, bf16[16,256]{1,0:T(8,128)(2,1)} %hk.1, ...), custom_call_target="tpu_custom_call" | custom-call | flops 1048576 | bytes 1048576 | tf_op jit(solution)/shard_map/pallas_call | solution.py:113
  2.8 32.9 %all_to_all.10.b = bf16[8,392,128]{2,1,0:T(8,128)(2,1)} all-to-all(bf16[8,392,128]{2,1,0:T(8,128)(2,1)} %get-tuple-element.13), channel_id=1, replica_groups=mesh['z'=8,'x'=4,'tp'=2,'job'=8] {'z'}, dimensions={0} | all-to-all | bytes 1605632 | tf_op jit(solution)/shard_map/all_to_all | solution.py:130
  35.7 3.0 %shard_map.140 = bf16[4,8,392,128]{3,2,1,0:T(8,128)(2,1)} custom-call(bf16[8,392,128]{2,1,0:T(8,128)(2,1)} %all_to_all.10.b), custom_call_target="tpu_custom_call" | custom-call | flops 1048576 | bytes 1048576 | tf_op jit(solution)/shard_map/pallas_call | solution.py:113
  38.8 4.1 %all-to-all-start.1 = ((bf16[4,8,392,128]{3,2,1,0:T(8,128)(2,1)}), bf16[4,8,392,128]{3,2,1,0:T(8,128)(2,1)S(1)}, u32[]{:S(2)}, u32[]{:S(2)}) async-start(bf16[4,8,392,128]{3,2,1,0:T(8,128)(2,1)} %shard_map.140), calls=%async_computation.1 | async-start | bytes 6422528 | tf_op jit(solution)/shard_map/all_to_all | solution.py:130
  42.9 4.9 %collective-permute-start.2 = (bf16[64,768]{1,0:T(8,128)(2,1)S(1)}, bf16[64,768]{1,0:T(8,128)(2,1)S(1)}, u32[]{:S(2)}, u32[]{:S(2)}) collective-permute-start(bf16[64,768]{1,0:T(8,128)(2,1)S(1)} %copy-done.4), channel_id=1, source_target_pairs={{0,32},{16,48},{32,0},{48,16},{1,33},{17,49},{33,1},{49,17},{2,34}... | collective-permute-start | bytes 294920 | tf_op jit(solution)/shard_map/ppermute | solution.py:126
  47.8 2.8 %collective-permute-start.1 = (bf16[64,768]{1,0:T(8,128)(2,1)S(1)}, bf16[64,768]{1,0:T(8,128)(2,1)S(1)}, u32[]{:S(2)}, u32[]{:S(2)}) collective-permute-start(bf16[64,768]{1,0:T(8,128)(2,1)S(1)} %copy-done.4), channel_id=1, source_target_pairs={{0,48},{16,0},{32,16},{48,32},{1,49},{17,1},{33,17},{49,33},{2,50}... | collective-permute-start | bytes 294920 | tf_op jit(solution)/shard_map/ppermute | solution.py:126
  50.6 2.5 %collective-permute-start = (bf16[64,768]{1,0:T(8,128)(2,1)S(1)}, bf16[64,768]{1,0:T(8,128)(2,1)}, u32[]{:S(2)}, u32[]{:S(2)}) collective-permute-start(bf16[64,768]{1,0:T(8,128)(2,1)S(1)} %copy-done.4), channel_id=1, source_target_pairs={{0,16},{16,32},{32,48},{48,0},{1,17},{17,33},{33,49},{49,1},{2,18}... | collective-permute-start | bytes 294920 | tf_op jit(solution)/shard_map/ppermute | solution.py:126
  53.1 27.6 %collective-permute-done.2.refs_3_ = bf16[64,768]{1,0:T(8,128)(2,1)S(1)} collective-permute-done((bf16[64,768]{1,0:T(8,128)(2,1)S(1)}, bf16[64,768]{1,0:T(8,128)(2,1)S(1)}, u32[]{:S(2)}, u32[]{:S(2)}) %collective-permute-start.2) | collective-permute-done | bytes 98336 | tf_op jit(solution)/shard_map/ppermute | solution.py:126
  81.9 2.0 %shard_map.139.refs_0_ = bf16[768,256]{1,0:T(8,128)(2,1)} custom-call(bf16[64,768]{1,0:T(8,128)(2,1)} %get-tuple-element.12.refs_0_, bf16[64,768]{1,0:T(8,128)(2,1)} %collective-permute-done.refs_1_, bf16[64,768]{1,0:T(8,128)(2,1)} %copy-done.6, bf16[64,768]{1,0:T(8,128)(2,1)} %copy-done.5), custom_call_target="tpu_custom_call" | custom-call | flops 1048576 | bytes 1048576 | tf_op jit(solution)/shard_map/pallas_call | solution.py:113
  83.9 1.9 %collective-permute-start.3 = (bf16[768,256]{1,0:T(8,128)(2,1)}, bf16[768,256]{1,0:T(8,128)(2,1)S(1)}, u32[]{:S(2)}, u32[]{:S(2)}) collective-permute-start(bf16[768,256]{1,0:T(8,128)(2,1)} %shard_map.139.refs_0_), channel_id=1, source_target_pairs={{0,64},{64,128},{128,192},{192,256},{256,320},{320,384},{384,448},... | collective-permute-start | bytes 1179656 | tf_op jit(solution)/shard_map/ppermute | solution.py:126
  85.8 4.6 %collective-permute-start.6 = (bf16[768,256]{1,0:T(8,128)(2,1)}, bf16[768,256]{1,0:T(8,128)(2,1)S(1)}, u32[]{:S(2)}, u32[]{:S(2)}) collective-permute-start(bf16[768,256]{1,0:T(8,128)(2,1)} %shard_map.139.refs_0_), channel_id=1, source_target_pairs={{0,448},{64,0},{128,64},{192,128},{256,192},{320,256},{384,320},{4... | collective-permute-start | bytes 1179656 | tf_op jit(solution)/shard_map/ppermute | solution.py:126
  90.4 3.4 %collective-permute-done.3.refs_1_ = bf16[768,256]{1,0:T(8,128)(2,1)S(1)} collective-permute-done((bf16[768,256]{1,0:T(8,128)(2,1)}, bf16[768,256]{1,0:T(8,128)(2,1)S(1)}, u32[]{:S(2)}, u32[]{:S(2)}) %collective-permute-start.3) | collective-permute-done | bytes 393248 | tf_op jit(solution)/shard_map/ppermute | solution.py:126
  93.8 1.9 %collective-permute-start.4 = (bf16[768,256]{1,0:T(8,128)(2,1)S(1)}, bf16[768,256]{1,0:T(8,128)(2,1)S(1)}, u32[]{:S(2)}, u32[]{:S(2)}) collective-permute-start(bf16[768,256]{1,0:T(8,128)(2,1)S(1)} %collective-permute-done.3.refs_1_), channel_id=1, source_target_pairs={{0,64},{64,128},{128,192},{192,256},{256,320},{320,384},{384,448},... | collective-permute-start | bytes 1179656 | tf_op jit(solution)/shard_map/ppermute | solution.py:126
  95.8 4.6 %collective-permute-start.7 = (bf16[768,256]{1,0:T(8,128)(2,1)S(1)}, bf16[768,256]{1,0:T(8,128)(2,1)}, u32[]{:S(2)}, u32[]{:S(2)}) collective-permute-start(bf16[768,256]{1,0:T(8,128)(2,1)S(1)} %collective-permute-done.6.refs_2_), channel_id=1, source_target_pairs={{0,448},{64,0},{128,64},{192,128},{256,192},{320,256},{384,320},{4... | collective-permute-start | bytes 1179656 | tf_op jit(solution)/shard_map/ppermute | solution.py:126
  100.3 3.2 %collective-permute-done.4.refs_3_ = bf16[768,256]{1,0:T(8,128)(2,1)S(1)} collective-permute-done((bf16[768,256]{1,0:T(8,128)(2,1)S(1)}, bf16[768,256]{1,0:T(8,128)(2,1)S(1)}, u32[]{:S(2)}, u32[]{:S(2)}) %collective-permute-start.4) | collective-permute-done | bytes 393248 | tf_op jit(solution)/shard_map/ppermute | solution.py:126
  103.6 1.9 %collective-permute-start.5 = (bf16[768,256]{1,0:T(8,128)(2,1)S(1)}, bf16[768,256]{1,0:T(8,128)(2,1)}, u32[]{:S(2)}, u32[]{:S(2)}) collective-permute-start(bf16[768,256]{1,0:T(8,128)(2,1)S(1)} %collective-permute-done.4.refs_3_), channel_id=1, source_target_pairs={{0,64},{64,128},{128,192},{192,256},{256,320},{320,384},{384,448},... | collective-permute-start | bytes 1179656 | tf_op jit(solution)/shard_map/ppermute | solution.py:126
  105.5 4.7 %collective-permute-start.8 = (bf16[768,256]{1,0:T(8,128)(2,1)}, bf16[768,256]{1,0:T(8,128)(2,1)}, u32[]{:S(2)}, u32[]{:S(2)}) collective-permute-start(bf16[768,256]{1,0:T(8,128)(2,1)} %collective-permute-done.7.refs_4_), channel_id=1, source_target_pairs={{0,448},{64,0},{128,64},{192,128},{256,192},{320,256},{384,320},{4... | collective-permute-start | bytes 1179656 | tf_op jit(solution)/shard_map/ppermute | solution.py:126
  110.2 3.5 %collective-permute-done.5.refs_0_ = bf16[768,256]{1,0:T(8,128)(2,1)} collective-permute-done((bf16[768,256]{1,0:T(8,128)(2,1)S(1)}, bf16[768,256]{1,0:T(8,128)(2,1)}, u32[]{:S(2)}, u32[]{:S(2)}) %collective-permute-start.5) | collective-permute-done | bytes 393248 | tf_op jit(solution)/shard_map/ppermute | solution.py:126
  113.7 1.9 %collective-permute-start.9 = (bf16[768,256]{1,0:T(8,128)(2,1)}, bf16[768,256]{1,0:T(8,128)(2,1)}, u32[]{:S(2)}, u32[]{:S(2)}) collective-permute-start(bf16[768,256]{1,0:T(8,128)(2,1)} %collective-permute-done.5.refs_0_), channel_id=1, source_target_pairs={{0,64},{64,128},{128,192},{192,256},{256,320},{320,384},{384,448},... | collective-permute-start | bytes 1179656 | tf_op jit(solution)/shard_map/ppermute | solution.py:126
  115.7 10.7 %collective-permute-start.10 = (bf16[32,32]{1,0:T(8,128)(2,1)S(1)}, bf16[32,32]{1,0:T(8,128)(2,1)S(1)}, u32[]{:S(2)}, u32[]{:S(2)}) collective-permute-start(bf16[32,32]{1,0:T(8,128)(2,1)S(1)} %bitcast.12), channel_id=1, source_target_pairs={{0,8},{8,0},{1,9},{9,1},{2,10},{10,2},{3,11},{11,3},{4,12},{12,4},... | collective-permute-start | bytes 6152 | tf_op jit(solution)/shard_map/ppermute | solution.py:213
  126.4 2.9 %shard_map.141 = (bf16[1024,2048]{1,0:T(8,128)(2,1)}, bf16[256,2048]{1,0:T(8,128)(2,1)}, bf16[256,2048]{1,0:T(8,128)(2,1)}) custom-call(bf16[768,256]{1,0:T(8,128)(2,1)} %shard_map.139.refs_0_, bf16[768,256]{1,0:T(8,128)(2,1)} %copy-done.1, bf16[768,256]{1,0:T(8,128)(2,1)} %copy-done.2, bf16[768,256]{1,0:T(8,128)(2,1)} %copy-done.3, ...), custom_call_target="tpu_custom_call" | custom-call | flops 1048576 | bytes 1048576 | tf_op jit(solution)/shard_map/pallas_call | solution.py:113
  129.3 3.8 %shard_map.142.refs_3_ = bf16[1024,2048]{1,0:T(8,128)(2,1)} custom-call(bf16[4,8,392,128]{3,2,1,0:T(8,128)(2,1)} %copy-done, bf16[1024,2048]{1,0:T(8,128)(2,1)} %get-tuple-element.14.rest_0_), custom_call_target="tpu_custom_call", output_to_operand_aliasing={{}: (1, {})} | custom-call | flops 1048576 | bytes 1048576 | tf_op jit(solution)/shard_map/pallas_call | solution.py:113
  133.1 2.3 %shard_map.143 = (bf16[1024,2048]{1,0:T(8,128)(2,1)}, bf16[256,2048]{1,0:T(8,128)(2,1)}, bf16[256,2048]{1,0:T(8,128)(2,1)}) custom-call(bf16[768,256]{1,0:T(8,128)(2,1)} %collective-permute-done.5.refs_0_, bf16[768,256]{1,0:T(8,128)(2,1)} %collective-permute-done.8.refs_1_, ...), custom_call_target="tpu_custom_call", output_to_operand_aliasing={{0}: (3, {}), {1}: (4, {}), {2}: (5, {})} | custom-call | flops 1048576 | bytes 1048576 | tf_op jit(solution)/shard_map/pallas_call | solution.py:113
  135.6 0.7 reshape.15
  (27 shorter events, 1.4 us)
Async XLA Ops:
  38.7 4.1 %copy-start.4 = (bf16[64,768]{1,0:T(8,128)(2,1)S(1)}, bf16[64,768]{1,0:T(8,128)(2,1)}, u32[]{:S(2)}) copy-start(bf16[64,768]{1,0:T(8,128)(2,1)} %get-tuple-element.12.refs_0_) | copy-start | bytes 294916
  38.8 76.9 %all-to-all-start.1 = ((bf16[4,8,392,128]{3,2,1,0:T(8,128)(2,1)}), bf16[4,8,392,128]{3,2,1,0:T(8,128)(2,1)S(1)}, u32[]{:S(2)}, u32[]{:S(2)}) async-start(bf16[4,8,392,128]{3,2,1,0:T(8,128)(2,1)} %shard_map.140), calls=%async_computation.1 | async-start | bytes 6422528 | tf_op jit(solution)/shard_map/all_to_all | solution.py:130
  42.9 37.8 %collective-permute-start.2 = (bf16[64,768]{1,0:T(8,128)(2,1)S(1)}, bf16[64,768]{1,0:T(8,128)(2,1)S(1)}, u32[]{:S(2)}, u32[]{:S(2)}) collective-permute-start(bf16[64,768]{1,0:T(8,128)(2,1)S(1)} %copy-done.4), channel_id=1, source_target_pairs={{0,32},{16,48},{32,0},{48,16},{1,33},{17,49},{33,1},{49,17},{2,34}... | collective-permute-start | bytes 294920 | tf_op jit(solution)/shard_map/ppermute | solution.py:126
  47.8 33.5 %collective-permute-start.1 = (bf16[64,768]{1,0:T(8,128)(2,1)S(1)}, bf16[64,768]{1,0:T(8,128)(2,1)S(1)}, u32[]{:S(2)}, u32[]{:S(2)}) collective-permute-start(bf16[64,768]{1,0:T(8,128)(2,1)S(1)} %copy-done.4), channel_id=1, source_target_pairs={{0,48},{16,0},{32,16},{48,32},{1,49},{17,1},{33,17},{49,33},{2,50}... | collective-permute-start | bytes 294920 | tf_op jit(solution)/shard_map/ppermute | solution.py:126
  50.6 30.7 %collective-permute-start = (bf16[64,768]{1,0:T(8,128)(2,1)S(1)}, bf16[64,768]{1,0:T(8,128)(2,1)}, u32[]{:S(2)}, u32[]{:S(2)}) collective-permute-start(bf16[64,768]{1,0:T(8,128)(2,1)S(1)} %copy-done.4), channel_id=1, source_target_pairs={{0,16},{16,32},{32,48},{48,0},{1,17},{17,33},{33,49},{49,1},{2,18}... | collective-permute-start | bytes 294920 | tf_op jit(solution)/shard_map/ppermute | solution.py:126
  80.7 0.6 copy-start.5
  81.3 0.6 copy-start.6
  83.9 9.9 %collective-permute-start.3 = (bf16[768,256]{1,0:T(8,128)(2,1)}, bf16[768,256]{1,0:T(8,128)(2,1)S(1)}, u32[]{:S(2)}, u32[]{:S(2)}) collective-permute-start(bf16[768,256]{1,0:T(8,128)(2,1)} %shard_map.139.refs_0_), channel_id=1, source_target_pairs={{0,64},{64,128},{128,192},{192,256},{256,320},{320,384},{384,448},... | collective-permute-start | bytes 1179656 | tf_op jit(solution)/shard_map/ppermute | solution.py:126
  85.8 9.9 %collective-permute-start.6 = (bf16[768,256]{1,0:T(8,128)(2,1)}, bf16[768,256]{1,0:T(8,128)(2,1)S(1)}, u32[]{:S(2)}, u32[]{:S(2)}) collective-permute-start(bf16[768,256]{1,0:T(8,128)(2,1)} %shard_map.139.refs_0_), channel_id=1, source_target_pairs={{0,448},{64,0},{128,64},{192,128},{256,192},{320,256},{384,320},{4... | collective-permute-start | bytes 1179656 | tf_op jit(solution)/shard_map/ppermute | solution.py:126
  93.8 19.9 %copy-start.1 = (bf16[768,256]{1,0:T(8,128)(2,1)}, bf16[768,256]{1,0:T(8,128)(2,1)S(1)}, u32[]{:S(2)}) copy-start(bf16[768,256]{1,0:T(8,128)(2,1)S(1)} %collective-permute-done.3.refs_1_) | copy-start | bytes 1179652
  93.8 9.7 %collective-permute-start.4 = (bf16[768,256]{1,0:T(8,128)(2,1)S(1)}, bf16[768,256]{1,0:T(8,128)(2,1)S(1)}, u32[]{:S(2)}, u32[]{:S(2)}) collective-permute-start(bf16[768,256]{1,0:T(8,128)(2,1)S(1)} %collective-permute-done.3.refs_1_), channel_id=1, source_target_pairs={{0,64},{64,128},{128,192},{192,256},{256,320},{320,384},{384,448},... | collective-permute-start | bytes 1179656 | tf_op jit(solution)/shard_map/ppermute | solution.py:126
  95.8 17.9 %copy-start.2 = (bf16[768,256]{1,0:T(8,128)(2,1)}, bf16[768,256]{1,0:T(8,128)(2,1)S(1)}, u32[]{:S(2)}) copy-start(bf16[768,256]{1,0:T(8,128)(2,1)S(1)} %collective-permute-done.6.refs_2_) | copy-start | bytes 1179652
  95.8 9.7 %collective-permute-start.7 = (bf16[768,256]{1,0:T(8,128)(2,1)S(1)}, bf16[768,256]{1,0:T(8,128)(2,1)}, u32[]{:S(2)}, u32[]{:S(2)}) collective-permute-start(bf16[768,256]{1,0:T(8,128)(2,1)S(1)} %collective-permute-done.6.refs_2_), channel_id=1, source_target_pairs={{0,448},{64,0},{128,64},{192,128},{256,192},{320,256},{384,320},{4... | collective-permute-start | bytes 1179656 | tf_op jit(solution)/shard_map/ppermute | solution.py:126
  103.5 10.2 %copy-start.3 = (bf16[768,256]{1,0:T(8,128)(2,1)}, bf16[768,256]{1,0:T(8,128)(2,1)S(1)}, u32[]{:S(2)}) copy-start(bf16[768,256]{1,0:T(8,128)(2,1)S(1)} %collective-permute-done.4.refs_3_) | copy-start | bytes 1179652
  103.6 10.1 %collective-permute-start.5 = (bf16[768,256]{1,0:T(8,128)(2,1)S(1)}, bf16[768,256]{1,0:T(8,128)(2,1)}, u32[]{:S(2)}, u32[]{:S(2)}) collective-permute-start(bf16[768,256]{1,0:T(8,128)(2,1)S(1)} %collective-permute-done.4.refs_3_), channel_id=1, source_target_pairs={{0,64},{64,128},{128,192},{192,256},{256,320},{320,384},{384,448},... | collective-permute-start | bytes 1179656 | tf_op jit(solution)/shard_map/ppermute | solution.py:126
  105.5 27.6 %collective-permute-start.8 = (bf16[768,256]{1,0:T(8,128)(2,1)}, bf16[768,256]{1,0:T(8,128)(2,1)}, u32[]{:S(2)}, u32[]{:S(2)}) collective-permute-start(bf16[768,256]{1,0:T(8,128)(2,1)} %collective-permute-done.7.refs_4_), channel_id=1, source_target_pairs={{0,448},{64,0},{128,64},{192,128},{256,192},{320,256},{384,320},{4... | collective-permute-start | bytes 1179656 | tf_op jit(solution)/shard_map/ppermute | solution.py:126
  113.7 19.4 %collective-permute-start.9 = (bf16[768,256]{1,0:T(8,128)(2,1)}, bf16[768,256]{1,0:T(8,128)(2,1)}, u32[]{:S(2)}, u32[]{:S(2)}) collective-permute-start(bf16[768,256]{1,0:T(8,128)(2,1)} %collective-permute-done.5.refs_0_), channel_id=1, source_target_pairs={{0,64},{64,128},{128,192},{192,256},{256,320},{320,384},{384,448},... | collective-permute-start | bytes 1179656 | tf_op jit(solution)/shard_map/ppermute | solution.py:126
  115.6 13.6 %copy-start = (bf16[4,8,392,128]{3,2,1,0:T(8,128)(2,1)}, bf16[4,8,392,128]{3,2,1,0:T(8,128)(2,1)S(1)}, u32[]{:S(2)}) copy-start(bf16[4,8,392,128]{3,2,1,0:T(8,128)(2,1)S(1)} %all-to-all-done.1.b) | copy-start | bytes 9633796
  115.7 19.7 %collective-permute-start.10 = (bf16[32,32]{1,0:T(8,128)(2,1)S(1)}, bf16[32,32]{1,0:T(8,128)(2,1)S(1)}, u32[]{:S(2)}, u32[]{:S(2)}) collective-permute-start(bf16[32,32]{1,0:T(8,128)(2,1)S(1)} %bitcast.12), channel_id=1, source_target_pairs={{0,8},{8,0},{1,9},{9,1},{2,10},{10,2},{3,11},{11,3},{4,12},{12,4},... | collective-permute-start | bytes 6152 | tf_op jit(solution)/shard_map/ppermute | solution.py:213

commit v2 on v1

v2 whole, which is shorter than its diff:
```python
import functools

import jax
import jax.numpy as jnp
from jax import lax
from jax.experimental import pallas as pl
from jax.experimental.pallas import tpu as pltpu
from jax.sharding import Mesh, PartitionSpec as P


mix_rate = 0.5
LANES = 128
NORM_ROWS = 8
A_Q = 2
B_CUTS = (6,)


def merged(t, l, h, lo, hi):
    low_high = lax.dot_general(
        l[...], h[:, lo:hi], (((0,), (0,)), ((), ())), preferred_element_type=jnp.float32
    )
    return (t[:, lo:hi].astype(jnp.float32) + mix_rate * low_high).astype(jnp.bfloat16)


def merge_kernel(tq, lq, hq, tk, lk, hk, tv, lv, hv, nt, ns, out_b, out_a):
    rows = tq.shape[0]
    w = merged(tq, lq, hq, A_Q * LANES, tq.shape[1])
    for d in range(out_b.shape[0]):
        for j in range(w.shape[1] // LANES):
            out_b[d, j * rows : (j + 1) * rows, :] = w[:, j * LANES : (j + 1) * LANES]
    at = 0
    for t, l, h, width in (
        (tk, lk, hk, tk.shape[1]),
        (tv, lv, hv, tv.shape[1]),
        (tq, lq, hq, A_Q * LANES),
    ):
        out_a[:rows, at : at + width] = merged(t, l, h, 0, width)
        at += width
    norm = nt[...] + ns[...]
    norm = jnp.concatenate([norm, jnp.zeros((1, LANES - norm.shape[1]), jnp.float32)], axis=1)
    norm = jnp.broadcast_to(norm, (NORM_ROWS, LANES)).astype(jnp.bfloat16)
    out_a[rows:, :LANES] = norm
    out_a[rows:, LANES:] = jnp.zeros((NORM_ROWS, out_a.shape[1] - LANES), jnp.bfloat16)


def turn_kernel(rows, part, a, out, out_norm):
    n, _, width = a.shape
    for j in range(width // LANES):
        block = jnp.concatenate(
            [a[x, :rows, j * LANES : (j + 1) * LANES] for x in range(n)], axis=0
        )
        out[j * LANES : (j + 1) * LANES, :] = block.T
    norm = jnp.concatenate([a[x, rows:, :part] for x in range(n)], axis=1)
    out_norm[...] = norm
    out[width:, : n * part] = norm
    out[width:, n * part :] = jnp.zeros((NORM_ROWS, out.shape[1] - n * part), jnp.bfloat16)


def place_b_kernel(first, cut, rows, b, *rest):
    out, held, sem = rest[-3:]
    nx, nz = b.shape[0], b.shape[1]
    wide = nx * rows
    copies = []
    for j in range(cut):
        for z in range(nz):
            block = jnp.concatenate(
                [b[x, z, j * rows : (j + 1) * rows, :] for x in range(nx)], axis=0
            )
            held[j * LANES : (j + 1) * LANES, z * wide : (z + 1) * wide] = block.T
        copy = pltpu.make_async_copy(
            held.at[pl.ds(j * LANES, LANES), :],
            out.at[pl.ds((first + j) * LANES, LANES), :],
            sem.at[j],
        )
        copy.start()
        copies.append(copy)
    for copy in copies:
        copy.wait()


def place_a(steps, nz, wide, kv, blocks, out_q, out_k, out_v, sem):
    me = lax.axis_index("z")
    end = 2 * kv + A_Q * LANES
    copies = []
    for i, (step, block) in enumerate(zip(steps, blocks)):
        z = lax.rem(me + (step + nz), nz)
        at = pl.ds(pl.multiple_of(z * wide, wide), wide)
        for s, (lo, hi, out) in enumerate(
            ((0, kv, out_k), (kv, 2 * kv, out_v), (2 * kv, end, out_q))
        ):
            copy = pltpu.make_async_copy(
                block.at[pl.ds(lo, hi - lo), :], out.at[pl.ds(0, hi - lo), at], sem.at[i, s]
            )
            copy.start()
            copies.append(copy)
    return copies


def early_kernel(steps, nz, wide, kv, *refs):
    n = len(steps)
    blocks, far = refs[:n], refs[n]
    out_q, out_k, out_v, out_n, held, sem = refs[n + 1 :]
    copies = place_a(steps, nz, wide, kv, blocks, out_q, out_k, out_v, sem)
    me = lax.axis_index("z")
    end = 2 * kv + A_Q * LANES
    lanes = held.shape[1]
    rows = [block[end:, :lanes] for block in blocks] + [far[...]]
    for step, row in zip(steps + (nz // 2,), rows):
        held[pl.ds(lax.rem(me + (step + nz), nz), 1), :] = row.astype(jnp.float32)[:1, :]
    out_n[...] = held[...].astype(out_n.dtype)
    for copy in copies:
        copy.wait()


def late_kernel(steps, nz, wide, kv, *refs):
    n = len(steps)
    copies = place_a(steps, nz, wide, kv, refs[:n], *refs[-4:])
    for copy in copies:
        copy.wait()


def norm_kernel(part, mine, other, out):
    m, o = mine[...].astype(jnp.float32), other[...].astype(jnp.float32)
    first = lax.axis_index("tp") == 0
    halves = (jnp.where(first, m, o), jnp.where(first, o, m))
    pieces = []
    for x in range(m.shape[1] // part):
        pieces += [half[:, x * part : (x + 1) * part] for half in halves]
    out[...] = jnp.concatenate(pieces, axis=1).astype(out.dtype)


def fan_kernel(b, out, sem):
    copies = [pltpu.make_async_copy(b, out.at[d], sem.at[d]) for d in range(out.shape[0])]
    for copy in copies:
        copy.start()
    for copy in copies:
        copy.wait()


VM = pl.BlockSpec(memory_space=pltpu.VMEM)
ANY = pl.BlockSpec(memory_space=pl.ANY)
HBM = pl.BlockSpec(memory_space=pltpu.HBM)


def call(kernel, ins, out_specs, out_shape, scratch=(), aliases={}, n_any=0, cost=1 << 20, vmem=16 << 20):
    return pl.pallas_call(
        kernel,
        in_specs=[VM] * (len(ins) - n_any) + [ANY] * n_any,
        out_specs=out_specs,
        out_shape=out_shape,
        scratch_shapes=list(scratch),
        input_output_aliases=aliases,
        compiler_params=pltpu.CompilerParams(vmem_limit_bytes=vmem),
        cost_estimate=pl.CostEstimate(flops=cost, bytes_accessed=cost, transcendentals=0),
    )(*ins)


def shift(a, axis, by):
    n = lax.axis_size(axis)
    return lax.ppermute(a, axis, [(i, (i + by) % n) for i in range(n)])


def spread(a, axis):
    return lax.all_to_all(a, axis, 0, 0, tiled=True)


def steps_of(tq, lq, hq, tk, lk, hk, tv, lv, hv, nt, ns):
    nz, nx = lax.axis_size("z"), lax.axis_size("x")
    rows, q_wide = tq.shape
    kv = tk.shape[1]
    wide = nx * rows
    a_wide = 2 * kv + A_Q * LANES
    bf = jnp.bfloat16
    low_q, low_k, low_v = lq.T, lk.T, lv.T
    part = nt.shape[0]
    b, a = call(
        merge_kernel,
        (tq, low_q, hq, tk, low_k, hk, tv, low_v, hv, nt[None], ns[None]),
        [VM, VM],
        [
            jax.ShapeDtypeStruct((nz, (q_wide // LANES - A_Q) * rows, LANES), bf),
            jax.ShapeDtypeStruct((rows + NORM_ROWS, a_wide), bf),
        ],
        vmem=None,
    )
    b1 = [spread(b, "z")]
    a = lax.all_gather(a, "x")
    own, own_norm = call(
        functools.partial(turn_kernel, rows, part),
        (a,),
        [VM, VM],
        [
            jax.ShapeDtypeStruct((a_wide + NORM_ROWS, wide), bf),
            jax.ShapeDtypeStruct((NORM_ROWS, nx * part), bf),
        ],
    )
    blocks = {0: own}
    for step in range(1, nz // 2):
        blocks[-step] = shift(blocks[1 - step], "z", 1)
        blocks[step] = shift(blocks[step - 1], "z", -1)
    blocks[-(nz // 2)] = shift(blocks[1 - nz // 2], "z", 1)
    b2 = []
    for b in b1:
        wide_b = call(
            fan_kernel,
            (b,),
            HBM,
            jax.ShapeDtypeStruct((nx, *b.shape), bf),
            scratch=[pltpu.SemaphoreType.DMA((nx,))],
        )
        b2.append(spread(wide_b, "x"))
    q_shape = jax.ShapeDtypeStruct((q_wide, nz * wide), bf)
    kv_shape = jax.ShapeDtypeStruct((kv, nz * wide), bf)

    def place_b(k, out_q):
        first = A_Q + sum(B_CUTS[:k])
        cut = B_CUTS[k]
        ins = (b2[k],) if out_q is None else (b2[k], out_q)
        return call(
            functools.partial(place_b_kernel, first, cut, rows),
            ins,
            ANY,
            q_shape,
            scratch=[pltpu.VMEM((cut * LANES, nz * wide), bf), pltpu.SemaphoreType.DMA((cut,))],
            aliases={} if out_q is None else {1: 0},
            n_any=len(ins) - 1,
        )

    half = nz // 2
    early = tuple(range(1 - half, half))
    far = shift(own_norm, "z", half)
    out_q, out_k, out_v, norm = call(
        functools.partial(early_kernel, early, nz, wide, kv),
        tuple(blocks[s] for s in early) + (far,),
        [ANY] * 3 + [VM],
        [q_shape, kv_shape, kv_shape, jax.ShapeDtypeStruct((nz, nx * part), bf)],
        scratch=[
            pltpu.VMEM((nz, nx * part), jnp.float32),
            pltpu.SemaphoreType.DMA((len(early), 3)),
        ],
    )
    other = lax.ppermute(norm, "tp", [(0, 1), (1, 0)])
    serve_norm = call(
        functools.partial(norm_kernel, part),
        (norm, other),
        VM,
        jax.ShapeDtypeStruct((nz, wide), bf),
    ).reshape(-1)
    for k in range(len(B_CUTS)):
        out_q = place_b(k, out_q)
    serve_query, serve_key, serve_value = call(
        functools.partial(late_kernel, (-half,), nz, wide, kv),
        (blocks[-half], out_q, out_k, out_v),
        [ANY] * 3,
        [q_shape, kv_shape, kv_shape],
        scratch=[pltpu.SemaphoreType.DMA((1, 3))],
        aliases={1 + i: i for i in range(3)},
        n_any=3,
    )
    return serve_query, serve_key, serve_value, serve_norm


def solution(mesh):
    rows, tp, job = mesh.devices.shape
    nx = 4
    fine = Mesh(mesh.devices.reshape(rows // nx, nx, tp, job), ("z", "x", "tp", "job"))
    r = ("job", "z", "x")
    w, low, high, vec = P(r, "tp"), P(r, None), P("job", "tp"), P(("job", "z", "x", "tp"))
    out_specs = (P(("job", "tp"), None),) * 3 + (P("job"),)
    return jax.shard_map(
        steps_of,
        mesh=fine,
        in_specs=(w, low, high) * 3 + (vec, vec),
        out_specs=out_specs,
        check_vma=False,
    )
```

time: 137 us -> 145 us (1.058)
  blocking collectives: 32.9 us -> 72.9 us
  waiting for transfers between devices: 38.4 us -> 17.9 us
  Pallas kernels: 16.1 us -> 8.03 us
  starting transfers between devices: 46.5 us -> 42.8 us
    all_gather x0 -> x1, blocking collectives: none -> 40.3 us  [steps_of(): a = lax.all_gather(a, 'x')]
    ppermute x10 -> x8, waiting for transfers between devices: 38.4 us -> 17.1 us  [shift(): return lax.ppermute(a, axis, [(i, (i + by) % n) for i in range(n)])]
    pallas_call x6 -> x7, Pallas kernels: 16.1 us -> 8.03 us  [call(): pl.pallas_call(kernel, in_specs=[VM] * (len(ins) - n_any) + [ANY] * n_any...]
    ppermute x10 -> x8, starting transfers between devices: 31.6 us -> 25.1 us  [shift(): return lax.ppermute(a, axis, [(i, (i + by) % n) for i in range(n)])]
    ppermute x1, starting transfers between devices: 10.7 us -> 13.7 us  [steps_of(): other = lax.ppermute(norm, 'tp', [(0, 1), (1, 0)])]
    unnamed x15 -> x5, local copies, waits for them, and re-layouts: 0.66 us -> 2.25 us
  transfers between devices with their start and end apart: 12 -> 10, of which waited for: 5 -> 5; matrix products, arithmetic and copies ran while one was open for 0% -> 0% of each run, Pallas kernels for 8% -> 3%
where the time goes in v2:
time: 145 us
  blocking collectives  72.9 us (50%)
  starting transfers between devices  42.8 us (30%)
  waiting for transfers between devices  17.9 us (12%)
  Pallas kernels  8.03 us (6%)
  local copies, waits for them, and re-layouts  2.25 us (2%)
    all_gather x1, blocking collectives, steps_of(): a = lax.all_gather(a, 'x')  40.3 us
    all_to_all x1, blocking collectives, spread(): return lax.all_to_all(a, axis, 0, 0, tiled=True)  32.6 us
    ppermute x8, starting transfers between devices, shift(): return lax.ppermute(a, axis, [(i, (i + by) % n) for i in range(n)])  25.1 us
    ppermute x8, waiting for transfers between devices, shift(): return lax.ppermute(a, axis, [(i, (i + by) % n) for i in range(n)])  17.1 us
    ppermute x1, starting transfers between devices, steps_of(): other = lax.ppermute(norm, 'tp', [(0, 1), (1, 0)])  13.7 us
    pallas_call x7, Pallas kernels, call(): pl.pallas_call(kernel, in_specs=[VM] * (len(ins) - n_any) + [ANY] * n_any...  8.03 us
    all_to_all x1, starting transfers between devices, spread(): return lax.all_to_all(a, axis, 0, 0, tiled=True)  4.01 us
  transfers between devices with their start and end apart: 10, of which 5 were waited for; matrix products, arithmetic and copies ran while one was open for 0% of the time, Pallas kernels for 3%

profile of v2, /device:TPU:1, one launch (start us, length us, event | category | flops | bytes accessed | tf_op | source)
XLA Modules:
  0.0 144.7 jit_solution(4403510114068744730)
XLA Ops:
  0.6 2.2 %shard_map.138 = (bf16[8,384,128]{2,1,0:T(8,128)(2,1)}, bf16[72,768]{1,0:T(8,128)(2,1)}) custom-call(bf16[64,1024]{1,0:T(8,128)(2,1)} %tq.1, bf16[16,64]{1,0:T(8,128)(2,1)} %bitcast.10, bf16[16,1024]{1,0:T(8,128)(2,1)} %hq.1, bf16[64,256]{1,0:T(8,128)(2,1)} %tk.1, bf16[16,64]{1,0:T(8,128)(2,1)} %bitcast.11, bf16[16,256]{1,0:T(8,128)(2,1)} %hk.1, ...), custom_call_target="tpu_custom_call" | custom-call | flops 1048576 | bytes 1048576 | tf_op jit(solution)/shard_map/pallas_call | solution.py:146
  2.8 32.6 %all_to_all.10.b = bf16[8,384,128]{2,1,0:T(8,128)(2,1)S(1)} all-to-all(bf16[8,384,128]{2,1,0:T(8,128)(2,1)} %get-tuple-element.17), channel_id=1, replica_groups=mesh['z'=8,'x'=4,'tp'=2,'job'=8] {'z'}, dimensions={0} | all-to-all | bytes 1572864 | tf_op jit(solution)/shard_map/all_to_all | solution.py:164
  35.4 0.3 shard_map.140
  35.7 1.6 %copy-done = bf16[4,8,384,128]{3,2,1,0:T(8,128)(2,1)} copy-done((bf16[4,8,384,128]{3,2,1,0:T(8,128)(2,1)}, bf16[4,8,384,128]{3,2,1,0:T(8,128)(2,1)S(1)}, u32[]{:S(2)}) %copy-start) | copy-done | bytes 3145752
  37.3 4.0 %all-to-all-start.1 = ((bf16[4,8,384,128]{3,2,1,0:T(8,128)(2,1)}), bf16[4,8,384,128]{3,2,1,0:T(8,128)(2,1)S(1)}, u32[]{:S(2)}, u32[]{:S(2)}) async-start(bf16[4,8,384,128]{3,2,1,0:T(8,128)(2,1)} %copy-done), calls=%async_computation.1 | async-start | bytes 6291456 | tf_op jit(solution)/shard_map/all_to_all | solution.py:164
  41.3 40.3 %all-gather = bf16[288,768]{1,0:T(8,128)(2,1)S(1)} all-gather(bf16[72,768]{1,0:T(8,128)(2,1)S(1)} %copy-done.1), channel_id=2, replica_groups=mesh['z'=8,'x'=4,'tp'=2,'job'=8] {'x'}, dimensions={0}, use_global_device_ids=true | all-gather | bytes 552960 | tf_op jit(solution)/shard_map/all_gather | solution.py:187
  81.8 1.9 %collective-permute-start = (bf16[776,256]{1,0:T(8,128)(2,1)S(1)}, bf16[776,256]{1,0:T(8,128)(2,1)S(1)}, u32[]{:S(2)}, u32[]{:S(2)}) collective-permute-start(bf16[776,256]{1,0:T(8,128)(2,1)S(1)} %get-tuple-element.16.refs_3_), channel_id=1, source_target_pairs={{0,64},{64,128},{128,192},{192,256},{256,320},{320,384},{384,448},... | collective-permute-start | bytes 1191944 | tf_op jit(solution)/shard_map/ppermute | solution.py:160
  83.8 4.6 %collective-permute-start.4 = (bf16[776,256]{1,0:T(8,128)(2,1)S(1)}, bf16[776,256]{1,0:T(8,128)(2,1)S(1)}, u32[]{:S(2)}, u32[]{:S(2)}) collective-permute-start(bf16[776,256]{1,0:T(8,128)(2,1)S(1)} %get-tuple-element.16.refs_3_), channel_id=1, source_target_pairs={{0,448},{64,0},{128,64},{192,128},{256,192},{320,256},{384,320},{4... | collective-permute-start | bytes 1191944 | tf_op jit(solution)/shard_map/ppermute | solution.py:160
  88.3 3.3 %collective-permute-done.refs_2_ = bf16[776,256]{1,0:T(8,128)(2,1)S(1)} collective-permute-done((bf16[776,256]{1,0:T(8,128)(2,1)S(1)}, bf16[776,256]{1,0:T(8,128)(2,1)S(1)}, u32[]{:S(2)}, u32[]{:S(2)}) %collective-permute-start) | collective-permute-done | bytes 397344 | tf_op jit(solution)/shard_map/ppermute | solution.py:160
  91.6 1.9 %collective-permute-start.1 = (bf16[776,256]{1,0:T(8,128)(2,1)S(1)}, bf16[776,256]{1,0:T(8,128)(2,1)S(1)}, u32[]{:S(2)}, u32[]{:S(2)}) collective-permute-start(bf16[776,256]{1,0:T(8,128)(2,1)S(1)} %collective-permute-done.refs_2_), channel_id=1, source_target_pairs={{0,64},{64,128},{128,192},{192,256},{256,320},{320,384},{384,448},... | collective-permute-start | bytes 1191944 | tf_op jit(solution)/shard_map/ppermute | solution.py:160
  93.5 4.6 %collective-permute-start.5 = (bf16[776,256]{1,0:T(8,128)(2,1)S(1)}, bf16[776,256]{1,0:T(8,128)(2,1)S(1)}, u32[]{:S(2)}, u32[]{:S(2)}) collective-permute-start(bf16[776,256]{1,0:T(8,128)(2,1)S(1)} %collective-permute-done.4.refs_4_), channel_id=1, source_target_pairs={{0,448},{64,0},{128,64},{192,128},{256,192},{320,256},{384,320},{4... | collective-permute-start | bytes 1191944 | tf_op jit(solution)/shard_map/ppermute | solution.py:160
  98.1 3.6 %collective-permute-done.1.refs_1_ = bf16[776,256]{1,0:T(8,128)(2,1)S(1)} collective-permute-done((bf16[776,256]{1,0:T(8,128)(2,1)S(1)}, bf16[776,256]{1,0:T(8,128)(2,1)S(1)}, u32[]{:S(2)}, u32[]{:S(2)}) %collective-permute-start.1) | collective-permute-done | bytes 397344 | tf_op jit(solution)/shard_map/ppermute | solution.py:160
  101.8 1.9 %collective-permute-start.2 = (bf16[776,256]{1,0:T(8,128)(2,1)S(1)}, bf16[776,256]{1,0:T(8,128)(2,1)S(1)}, u32[]{:S(2)}, u32[]{:S(2)}) collective-permute-start(bf16[776,256]{1,0:T(8,128)(2,1)S(1)} %collective-permute-done.1.refs_1_), channel_id=1, source_target_pairs={{0,64},{64,128},{128,192},{192,256},{256,320},{320,384},{384,448},... | collective-permute-start | bytes 1191944 | tf_op jit(solution)/shard_map/ppermute | solution.py:160
  103.7 4.8 %collective-permute-start.6 = (bf16[776,256]{1,0:T(8,128)(2,1)S(1)}, bf16[776,256]{1,0:T(8,128)(2,1)S(1)}, u32[]{:S(2)}, u32[]{:S(2)}) collective-permute-start(bf16[776,256]{1,0:T(8,128)(2,1)S(1)} %collective-permute-done.5.refs_5_), channel_id=1, source_target_pairs={{0,448},{64,0},{128,64},{192,128},{256,192},{320,256},{384,320},{4... | collective-permute-start | bytes 1191944 | tf_op jit(solution)/shard_map/ppermute | solution.py:160
  108.5 4.5 %collective-permute-done.2.refs_0_ = bf16[776,256]{1,0:T(8,128)(2,1)S(1)} collective-permute-done((bf16[776,256]{1,0:T(8,128)(2,1)S(1)}, bf16[776,256]{1,0:T(8,128)(2,1)S(1)}, u32[]{:S(2)}, u32[]{:S(2)}) %collective-permute-start.2) | collective-permute-done | bytes 397344 | tf_op jit(solution)/shard_map/ppermute | solution.py:160
  113.0 1.9 %collective-permute-start.3 = (bf16[776,256]{1,0:T(8,128)(2,1)S(1)}, bf16[776,256]{1,0:T(8,128)(2,1)}, u32[]{:S(2)}, u32[]{:S(2)}) collective-permute-start(bf16[776,256]{1,0:T(8,128)(2,1)S(1)} %collective-permute-done.2.refs_0_), channel_id=1, source_target_pairs={{0,64},{64,128},{128,192},{192,256},{256,320},{320,384},{384,448},... | collective-permute-start | bytes 1191944 | tf_op jit(solution)/shard_map/ppermute | solution.py:160
  115.0 3.5 %collective-permute-start.7 = (bf16[8,128]{1,0:T(8,128)(2,1)S(1)}, bf16[8,128]{1,0:T(8,128)(2,1)S(1)}, u32[]{:S(2)}, u32[]{:S(2)}) collective-permute-start(bf16[8,128]{1,0:T(8,128)(2,1)S(1)} %get-tuple-element.18), channel_id=1, source_target_pairs={{0,256},{64,320},{128,384},{192,448},{256,0},{320,64},{384,128},{4... | collective-permute-start | bytes 6152 | tf_op jit(solution)/shard_map/ppermute | solution.py:160
  118.5 5.7 %collective-permute-done.7.refs_7_ = bf16[8,128]{1,0:T(8,128)(2,1)S(1)} collective-permute-done((bf16[8,128]{1,0:T(8,128)(2,1)S(1)}, bf16[8,128]{1,0:T(8,128)(2,1)S(1)}, u32[]{:S(2)}, u32[]{:S(2)}) %collective-permute-start.7) | collective-permute-done | bytes 2080 | tf_op jit(solution)/shard_map/ppermute | solution.py:160
  124.1 1.7 %shard_map.141 = (bf16[1024,2048]{1,0:T(8,128)(2,1)}, bf16[256,2048]{1,0:T(8,128)(2,1)}, bf16[256,2048]{1,0:T(8,128)(2,1)}, bf16[8,128]{1,0:T(8,128)(2,1)S(1)}) custom-call(bf16[776,256]{1,0:T(8,128)(2,1)S(1)} %collective-permute-done.2.refs_0_, bf16[776,256]{1,0:T(8,128)(2,1)S(1)} %collective-permute-done.1.refs_1_, ...), custom_call_target="tpu_custom_call" | custom-call | flops 1048576 | bytes 1048576 | tf_op jit(solution)/shard_map/pallas_call | solution.py:146
  125.9 13.7 %collective-permute-start.8 = (bf16[8,128]{1,0:T(8,128)(2,1)S(1)}, bf16[8,128]{1,0:T(8,128)(2,1)S(1)}, u32[]{:S(2)}, u32[]{:S(2)}) collective-permute-start(bf16[8,128]{1,0:T(8,128)(2,1)S(1)} %get-tuple-element.25.mine), channel_id=1, source_target_pairs={{0,8},{8,0},{1,9},{9,1},{2,10},{10,2},{3,11},{11,3},{4,12},{12,4},... | collective-permute-start | bytes 6152 | tf_op jit(solution)/shard_map/ppermute | solution.py:242
  139.5 0.8 collective-permute-done.8.other
  140.4 0.6 copy.19
  141.0 1.9 %shard_map.142.refs_1_ = bf16[1024,2048]{1,0:T(8,128)(2,1)} custom-call(bf16[4,8,384,128]{3,2,1,0:T(8,128)(2,1)S(1)} %all-to-all-done.1.b, bf16[1024,2048]{1,0:T(8,128)(2,1)} %get-tuple-element.19.rest_0_), custom_call_target="tpu_custom_call", output_to_operand_aliasing={{}: (1, {})} | custom-call | flops 1048576 | bytes 1048576 | tf_op jit(solution)/shard_map/pallas_call | solution.py:146
  142.9 1.8 %shard_map.143 = (bf16[1024,2048]{1,0:T(8,128)(2,1)}, bf16[256,2048]{1,0:T(8,128)(2,1)}, bf16[256,2048]{1,0:T(8,128)(2,1)}) custom-call(bf16[776,256]{1,0:T(8,128)(2,1)} %collective-permute-done.3.refs_0_, bf16[1024,2048]{1,0:T(8,128)(2,1)} %shard_map.142.refs_1_, ...), custom_call_target="tpu_custom_call", output_to_operand_aliasing={{0}: (1, {}), {1}: (2, {}), {2}: (3, {})} | custom-call | flops 1048576 | bytes 1048576 | tf_op jit(solution)/shard_map/pallas_call | solution.py:146
  (10 shorter events, 0.3 us)
Async XLA Ops:
  35.4 5.9 %copy-start.1 = (bf16[72,768]{1,0:T(8,128)(2,1)S(1)}, bf16[72,768]{1,0:T(8,128)(2,1)}, u32[]{:S(2)}) copy-start(bf16[72,768]{1,0:T(8,128)(2,1)} %get-tuple-element.15) | copy-start | bytes 331780
  35.7 1.7 %copy-start = (bf16[4,8,384,128]{3,2,1,0:T(8,128)(2,1)}, bf16[4,8,384,128]{3,2,1,0:T(8,128)(2,1)S(1)}, u32[]{:S(2)}) copy-start(bf16[4,8,384,128]{3,2,1,0:T(8,128)(2,1)S(1)} %shard_map.140) | copy-start | bytes 9437188
  37.3 103.7 %all-to-all-start.1 = ((bf16[4,8,384,128]{3,2,1,0:T(8,128)(2,1)}), bf16[4,8,384,128]{3,2,1,0:T(8,128)(2,1)S(1)}, u32[]{:S(2)}, u32[]{:S(2)}) async-start(bf16[4,8,384,128]{3,2,1,0:T(8,128)(2,1)} %copy-done), calls=%async_computation.1 | async-start | bytes 6291456 | tf_op jit(solution)/shard_map/all_to_all | solution.py:164
  81.8 9.8 %collective-permute-start = (bf16[776,256]{1,0:T(8,128)(2,1)S(1)}, bf16[776,256]{1,0:T(8,128)(2,1)S(1)}, u32[]{:S(2)}, u32[]{:S(2)}) collective-permute-start(bf16[776,256]{1,0:T(8,128)(2,1)S(1)} %get-tuple-element.16.refs_3_), channel_id=1, source_target_pairs={{0,64},{64,128},{128,192},{192,256},{256,320},{320,384},{384,448},... | collective-permute-start | bytes 1191944 | tf_op jit(solution)/shard_map/ppermute | solution.py:160
  83.8 9.8 %collective-permute-start.4 = (bf16[776,256]{1,0:T(8,128)(2,1)S(1)}, bf16[776,256]{1,0:T(8,128)(2,1)S(1)}, u32[]{:S(2)}, u32[]{:S(2)}) collective-permute-start(bf16[776,256]{1,0:T(8,128)(2,1)S(1)} %get-tuple-element.16.refs_3_), channel_id=1, source_target_pairs={{0,448},{64,0},{128,64},{192,128},{256,192},{320,256},{384,320},{4... | collective-permute-start | bytes 1191944 | tf_op jit(solution)/shard_map/ppermute | solution.py:160
  91.6 10.1 %collective-permute-start.1 = (bf16[776,256]{1,0:T(8,128)(2,1)S(1)}, bf16[776,256]{1,0:T(8,128)(2,1)S(1)}, u32[]{:S(2)}, u32[]{:S(2)}) collective-permute-start(bf16[776,256]{1,0:T(8,128)(2,1)S(1)} %collective-permute-done.refs_2_), channel_id=1, source_target_pairs={{0,64},{64,128},{128,192},{192,256},{256,320},{320,384},{384,448},... | collective-permute-start | bytes 1191944 | tf_op jit(solution)/shard_map/ppermute | solution.py:160
  93.5 10.1 %collective-permute-start.5 = (bf16[776,256]{1,0:T(8,128)(2,1)S(1)}, bf16[776,256]{1,0:T(8,128)(2,1)S(1)}, u32[]{:S(2)}, u32[]{:S(2)}) collective-permute-start(bf16[776,256]{1,0:T(8,128)(2,1)S(1)} %collective-permute-done.4.refs_4_), channel_id=1, source_target_pairs={{0,448},{64,0},{128,64},{192,128},{256,192},{320,256},{384,320},{4... | collective-permute-start | bytes 1191944 | tf_op jit(solution)/shard_map/ppermute | solution.py:160
  101.8 11.3 %collective-permute-start.2 = (bf16[776,256]{1,0:T(8,128)(2,1)S(1)}, bf16[776,256]{1,0:T(8,128)(2,1)S(1)}, u32[]{:S(2)}, u32[]{:S(2)}) collective-permute-start(bf16[776,256]{1,0:T(8,128)(2,1)S(1)} %collective-permute-done.1.refs_1_), channel_id=1, source_target_pairs={{0,64},{64,128},{128,192},{192,256},{256,320},{320,384},{384,448},... | collective-permute-start | bytes 1191944 | tf_op jit(solution)/shard_map/ppermute | solution.py:160
  103.7 20.5 %collective-permute-start.6 = (bf16[776,256]{1,0:T(8,128)(2,1)S(1)}, bf16[776,256]{1,0:T(8,128)(2,1)S(1)}, u32[]{:S(2)}, u32[]{:S(2)}) collective-permute-start(bf16[776,256]{1,0:T(8,128)(2,1)S(1)} %collective-permute-done.5.refs_5_), channel_id=1, source_target_pairs={{0,448},{64,0},{128,64},{192,128},{256,192},{320,256},{384,320},{4... | collective-permute-start | bytes 1191944 | tf_op jit(solution)/shard_map/ppermute | solution.py:160
  113.0 29.9 %collective-permute-start.3 = (bf16[776,256]{1,0:T(8,128)(2,1)S(1)}, bf16[776,256]{1,0:T(8,128)(2,1)}, u32[]{:S(2)}, u32[]{:S(2)}) collective-permute-start(bf16[776,256]{1,0:T(8,128)(2,1)S(1)} %collective-permute-done.2.refs_0_), channel_id=1, source_target_pairs={{0,64},{64,128},{128,192},{192,256},{256,320},{320,384},{384,448},... | collective-permute-start | bytes 1191944 | tf_op jit(solution)/shard_map/ppermute | solution.py:160
  115.0 9.2 %collective-permute-start.7 = (bf16[8,128]{1,0:T(8,128)(2,1)S(1)}, bf16[8,128]{1,0:T(8,128)(2,1)S(1)}, u32[]{:S(2)}, u32[]{:S(2)}) collective-permute-start(bf16[8,128]{1,0:T(8,128)(2,1)S(1)} %get-tuple-element.18), channel_id=1, source_target_pairs={{0,256},{64,320},{128,384},{192,448},{256,0},{320,64},{384,128},{4... | collective-permute-start | bytes 6152 | tf_op jit(solution)/shard_map/ppermute | solution.py:160
  125.9 14.5 %collective-permute-start.8 = (bf16[8,128]{1,0:T(8,128)(2,1)S(1)}, bf16[8,128]{1,0:T(8,128)(2,1)S(1)}, u32[]{:S(2)}, u32[]{:S(2)}) collective-permute-start(bf16[8,128]{1,0:T(8,128)(2,1)S(1)} %get-tuple-element.25.mine), channel_id=1, source_target_pairs={{0,8},{8,0},{1,9},{9,1},{2,10},{10,2},{3,11},{11,3},{4,12},{12,4},... | collective-permute-start | bytes 6152 | tf_op jit(solution)/shard_map/ppermute | solution.py:242

commit v3 on v2

--- a/solution.py
+++ b/solution.py
@@ -12,7 +12,6 @@
 LANES = 128
 NORM_ROWS = 8
 A_Q = 2
-B_CUTS = (6,)
 
 
 def merged(t, l, h, lo, hi):
@@ -56,26 +55,36 @@
     out[width:, n * part :] = jnp.zeros((NORM_ROWS, out.shape[1] - n * part), jnp.bfloat16)
 
 
-def place_b_kernel(first, cut, rows, b, *rest):
+def place_b_kernel(first, cut, rows, nx, own, below, above, far_low, far_high, *rest):
     out, held, sem = rest[-3:]
-    nx, nz = b.shape[0], b.shape[1]
+    nz = own.shape[0]
     wide = nx * rows
-    copies = []
-    for j in range(cut):
-        for z in range(nz):
-            block = jnp.concatenate(
-                [b[x, z, j * rows : (j + 1) * rows, :] for x in range(nx)], axis=0
-            )
-            held[j * LANES : (j + 1) * LANES, z * wide : (z + 1) * wide] = block.T
-        copy = pltpu.make_async_copy(
+    half = nz // 2
+
+    def piece(step, z, at):
+        if step == nx // 2:
+            return far_low[z, at, :] if z < half else far_high[z - half, at, :]
+        return {0: own, 1: above, nx - 1: below}[step][z, at, :]
+
+    def turn_all(me):
+        for j in range(cut):
+            at = slice(j * rows, (j + 1) * rows)
+            for z in range(nz):
+                block = jnp.concatenate([piece((x - me) % nx, z, at) for x in range(nx)], axis=0)
+                held[j * LANES : (j + 1) * LANES, z * wide : (z + 1) * wide] = block.T
+            row_copy(j).start()
+
+    def row_copy(j):
+        return pltpu.make_async_copy(
             held.at[pl.ds(j * LANES, LANES), :],
             out.at[pl.ds((first + j) * LANES, LANES), :],
             sem.at[j],
         )
-        copy.start()
-        copies.append(copy)
-    for copy in copies:
-        copy.wait()
+
+    for me in range(nx):
+        pl.when(lax.axis_index("x") == me)(functools.partial(turn_all, me))
+    for j in range(cut):
+        row_copy(j).wait()
 
 
 def place_a(steps, nz, wide, kv, blocks, out_q, out_k, out_v, sem):
@@ -129,17 +138,8 @@
     out[...] = jnp.concatenate(pieces, axis=1).astype(out.dtype)
 
 
-def fan_kernel(b, out, sem):
-    copies = [pltpu.make_async_copy(b, out.at[d], sem.at[d]) for d in range(out.shape[0])]
-    for copy in copies:
-        copy.start()
-    for copy in copies:
-        copy.wait()
-
-
 VM = pl.BlockSpec(memory_space=pltpu.VMEM)
 ANY = pl.BlockSpec(memory_space=pl.ANY)
-HBM = pl.BlockSpec(memory_space=pltpu.HBM)
 
 
 def call(kernel, ins, out_specs, out_shape, scratch=(), aliases={}, n_any=0, cost=1 << 20, vmem=16 << 20):
@@ -183,7 +183,7 @@
         ],
         vmem=None,
     )
-    b1 = [spread(b, "z")]
+    b = spread(b, "z")
     a = lax.all_gather(a, "x")
     own, own_norm = call(
         functools.partial(turn_kernel, rows, part),
@@ -199,32 +199,12 @@
         blocks[-step] = shift(blocks[1 - step], "z", 1)
         blocks[step] = shift(blocks[step - 1], "z", -1)
     blocks[-(nz // 2)] = shift(blocks[1 - nz // 2], "z", 1)
-    b2 = []
-    for b in b1:
-        wide_b = call(
-            fan_kernel,
-            (b,),
-            HBM,
-            jax.ShapeDtypeStruct((nx, *b.shape), bf),
-            scratch=[pltpu.SemaphoreType.DMA((nx,))],
-        )
-        b2.append(spread(wide_b, "x"))
+    b_p = shift(b, "x", 1)
+    b_m = shift(b, "x", -1)
+    b_rp = shift(b_p[: nz // 2], "x", 1)
+    b_rm = shift(b_m[nz // 2 :], "x", -1)
     q_shape = jax.ShapeDtypeStruct((q_wide, nz * wide), bf)
     kv_shape = jax.ShapeDtypeStruct((kv, nz * wide), bf)
-
-    def place_b(k, out_q):
-        first = A_Q + sum(B_CUTS[:k])
-        cut = B_CUTS[k]
-        ins = (b2[k],) if out_q is None else (b2[k], out_q)
-        return call(
-            functools.partial(place_b_kernel, first, cut, rows),
-            ins,
-            ANY,
-            q_shape,
-            scratch=[pltpu.VMEM((cut * LANES, nz * wide), bf), pltpu.SemaphoreType.DMA((cut,))],
-            aliases={} if out_q is None else {1: 0},
-            n_any=len(ins) - 1,
-        )
 
     half = nz // 2
     early = tuple(range(1 - half, half))
@@ -246,8 +226,19 @@
         VM,
         jax.ShapeDtypeStruct((nz, wide), bf),
     ).reshape(-1)
-    for k in range(len(B_CUTS)):
-        out_q = place_b(k, out_q)
+    cut = q_wide // LANES - A_Q
+    out_q = call(
+        functools.partial(place_b_kernel, A_Q, cut, rows, nx),
+        (b, b_p, b_m, b_rp, b_rm, out_q),
+        ANY,
+        q_shape,
+        scratch=[
+            pltpu.VMEM((cut * LANES, nz * wide), bf),
+            pltpu.SemaphoreType.DMA((cut,)),
+        ],
+        aliases={5: 0},
+        n_any=1,
+    )
     serve_query, serve_key, serve_value = call(
         functools.partial(late_kernel, (-half,), nz, wide, kv),
         (blocks[-half], out_q, out_k, out_v),

time: 145 us -> 96.1 us (0.66)
  blocking collectives: 72.9 us -> 11.6 us
  starting transfers between devices: 42.8 us -> 55.9 us
  waiting for transfers between devices: 17.9 us -> 19.8 us
  local copies, waits for them, and re-layouts: 2.25 us -> 0.66 us
    all_to_all x1 -> x0, blocking collectives: 32.6 us -> none  [spread(): return lax.all_to_all(a, axis, 0, 0, tiled=True)]
    all_gather x1, blocking collectives: 40.3 us -> 11.6 us  [steps_of(): a = lax.all_gather(a, 'x')]
    ppermute x8 -> x12, starting transfers between devices: 25.1 us -> 38.4 us  [shift(): return lax.ppermute(a, axis, [(i, (i + by) % n) for i in range(n)])]
    ppermute x1, starting transfers between devices: 13.7 us -> 6.59 us  [steps_of(): other = lax.ppermute(norm, 'tp', [(0, 1), (1, 0)])]
    all_to_all x1, starting transfers between devices: 4.01 us -> 10.9 us  [spread(): return lax.all_to_all(a, axis, 0, 0, tiled=True)]
    ppermute x8 -> x12, waiting for transfers between devices: 17.1 us -> 19 us  [shift(): return lax.ppermute(a, axis, [(i, (i + by) % n) for i in range(n)])]
    unnamed x5 -> x1, local copies, waits for them, and re-layouts: 2.25 us -> 0.6 us
    pallas_call x7 -> x6, Pallas kernels: 8.03 us -> 6.8 us  [call(): pl.pallas_call(kernel, in_specs=[VM] * (len(ins) - n_any) + [ANY] * n_any...]
  transfers between devices with their start and end apart: 10 -> 14, of which waited for: 5 -> 6; matrix products, arithmetic and copies ran while one was open for 0% -> 1% of each run, Pallas kernels for 3% -> 4%
where the time goes in v3:
time: 96.1 us; the launch traced here: 95.6 us
  starting transfers between devices  55.9 us (58%)
  waiting for transfers between devices  19.8 us (21%)
  blocking collectives  11.6 us (12%)
  Pallas kernels  6.8 us (7%)
    ppermute x12, starting transfers between devices, shift(): return lax.ppermute(a, axis, [(i, (i + by) % n) for i in range(n)])  38.4 us
    ppermute x12, waiting for transfers between devices, shift(): return lax.ppermute(a, axis, [(i, (i + by) % n) for i in range(n)])  19 us
    all_gather x1, blocking collectives, steps_of(): a = lax.all_gather(a, 'x')  11.6 us
    all_to_all x1, starting transfers between devices, spread(): return lax.all_to_all(a, axis, 0, 0, tiled=True)  10.9 us
    pallas_call x6, Pallas kernels, call(): pl.pallas_call(kernel, in_specs=[VM] * (len(ins) - n_any) + [ANY] * n_any...  6.8 us
    ppermute x1, starting transfers between devices, steps_of(): other = lax.ppermute(norm, 'tp', [(0, 1), (1, 0)])  6.59 us
  transfers between devices with their start and end apart: 14, of which 6 were waited for; matrix products, arithmetic and copies ran while one was open for 1% of the time, Pallas kernels for 4%

profile of v3, /device:TPU:1, one launch (start us, length us, event | category | flops | bytes accessed | tf_op | source)
XLA Modules:
  0.0 95.6 jit_solution(14445895417237511202)
XLA Ops:
  0.6 2.2 %shard_map.138 = (bf16[8,384,128]{2,1,0:T(8,128)(2,1)}, bf16[72,768]{1,0:T(8,128)(2,1)}) custom-call(bf16[64,1024]{1,0:T(8,128)(2,1)} %tq.1, bf16[16,64]{1,0:T(8,128)(2,1)} %bitcast.10, bf16[16,1024]{1,0:T(8,128)(2,1)} %hq.1, bf16[64,256]{1,0:T(8,128)(2,1)} %tk.1, bf16[16,64]{1,0:T(8,128)(2,1)} %bitcast.11, bf16[16,256]{1,0:T(8,128)(2,1)} %hk.1, ...), custom_call_target="tpu_custom_call" | custom-call | flops 1048576 | bytes 1048576 | tf_op jit(solution)/shard_map/pallas_call | solution.py:146
  2.8 10.9 %all-to-all-start = ((bf16[8,384,128]{2,1,0:T(8,128)(2,1)}), bf16[8,384,128]{2,1,0:T(8,128)(2,1)S(1)}, u32[]{:S(2)}, u32[]{:S(2)}) async-start(bf16[8,384,128]{2,1,0:T(8,128)(2,1)} %get-tuple-element.17), calls=%async_computation | async-start | bytes 1572864 | tf_op jit(solution)/shard_map/all_to_all | solution.py:164
  13.7 11.6 %all-gather = bf16[288,768]{1,0:T(8,128)(2,1)S(1)} all-gather(bf16[72,768]{1,0:T(8,128)(2,1)} %get-tuple-element.15), channel_id=2, replica_groups=mesh['z'=8,'x'=4,'tp'=2,'job'=8] {'x'}, dimensions={0}, use_global_device_ids=true | all-gather | bytes 552960 | tf_op jit(solution)/shard_map/all_gather | solution.py:187
  25.4 3.3 %collective-permute-start = (bf16[776,256]{1,0:T(8,128)(2,1)S(1)}, bf16[776,256]{1,0:T(8,128)(2,1)S(1)}, u32[]{:S(2)}, u32[]{:S(2)}) collective-permute-start(bf16[776,256]{1,0:T(8,128)(2,1)S(1)} %get-tuple-element.16.refs_3_), channel_id=1, source_target_pairs={{0,64},{64,128},{128,192},{192,256},{256,320},{320,384},{384,448},... | collective-permute-start | bytes 1191944 | tf_op jit(solution)/shard_map/ppermute | solution.py:160
  28.7 3.5 %collective-permute-start.8 = (bf16[776,256]{1,0:T(8,128)(2,1)S(1)}, bf16[776,256]{1,0:T(8,128)(2,1)S(1)}, u32[]{:S(2)}, u32[]{:S(2)}) collective-permute-start(bf16[776,256]{1,0:T(8,128)(2,1)S(1)} %get-tuple-element.16.refs_3_), channel_id=1, source_target_pairs={{0,448},{64,0},{128,64},{192,128},{256,192},{320,256},{384,320},{4... | collective-permute-start | bytes 1191944 | tf_op jit(solution)/shard_map/ppermute | solution.py:160
  32.2 10.7 %collective-permute-done.refs_2_ = bf16[776,256]{1,0:T(8,128)(2,1)S(1)} collective-permute-done((bf16[776,256]{1,0:T(8,128)(2,1)S(1)}, bf16[776,256]{1,0:T(8,128)(2,1)S(1)}, u32[]{:S(2)}, u32[]{:S(2)}) %collective-permute-start) | collective-permute-done | bytes 397344 | tf_op jit(solution)/shard_map/ppermute | solution.py:160
  42.9 1.9 %collective-permute-start.1 = (bf16[776,256]{1,0:T(8,128)(2,1)S(1)}, bf16[776,256]{1,0:T(8,128)(2,1)S(1)}, u32[]{:S(2)}, u32[]{:S(2)}) collective-permute-start(bf16[776,256]{1,0:T(8,128)(2,1)S(1)} %collective-permute-done.refs_2_), channel_id=1, source_target_pairs={{0,64},{64,128},{128,192},{192,256},{256,320},{320,384},{384,448},... | collective-permute-start | bytes 1191944 | tf_op jit(solution)/shard_map/ppermute | solution.py:160
  44.9 3.2 %collective-permute-start.5 = (bf16[8,384,128]{2,1,0:T(8,128)(2,1)S(1)}, bf16[8,384,128]{2,1,0:T(8,128)(2,1)S(1)}, u32[]{:S(2)}, u32[]{:S(2)}) collective-permute-start(bf16[8,384,128]{2,1,0:T(8,128)(2,1)S(1)} %all-to-all-done.own), channel_id=1, source_target_pairs={{0,48},{16,0},{32,16},{48,32},{1,49},{17,1},{33,17},{49,33},{2,50}... | collective-permute-start | bytes 2359304 | tf_op jit(solution)/shard_map/ppermute | solution.py:160
  48.0 2.1 %collective-permute-start.4 = (bf16[8,384,128]{2,1,0:T(8,128)(2,1)S(1)}, bf16[8,384,128]{2,1,0:T(8,128)(2,1)S(1)}, u32[]{:S(2)}, u32[]{:S(2)}) collective-permute-start(bf16[8,384,128]{2,1,0:T(8,128)(2,1)S(1)} %all-to-all-done.own), channel_id=1, source_target_pairs={{0,16},{16,32},{32,48},{48,0},{1,17},{17,33},{33,49},{49,1},{2,18}... | collective-permute-start | bytes 2359304 | tf_op jit(solution)/shard_map/ppermute | solution.py:160
  50.2 4.6 %collective-permute-start.9 = (bf16[776,256]{1,0:T(8,128)(2,1)S(1)}, bf16[776,256]{1,0:T(8,128)(2,1)S(1)}, u32[]{:S(2)}, u32[]{:S(2)}) collective-permute-start(bf16[776,256]{1,0:T(8,128)(2,1)S(1)} %collective-permute-done.8.refs_4_), channel_id=1, source_target_pairs={{0,448},{64,0},{128,64},{192,128},{256,192},{320,256},{384,320},{4... | collective-permute-start | bytes 1191944 | tf_op jit(solution)/shard_map/ppermute | solution.py:160
  54.8 0.9 collective-permute-done.1.refs_1_
  55.7 1.9 %collective-permute-start.2 = (bf16[776,256]{1,0:T(8,128)(2,1)S(1)}, bf16[776,256]{1,0:T(8,128)(2,1)S(1)}, u32[]{:S(2)}, u32[]{:S(2)}) collective-permute-start(bf16[776,256]{1,0:T(8,128)(2,1)S(1)} %collective-permute-done.1.refs_1_), channel_id=1, source_target_pairs={{0,64},{64,128},{128,192},{192,256},{256,320},{320,384},{384,448},... | collective-permute-start | bytes 1191944 | tf_op jit(solution)/shard_map/ppermute | solution.py:160
  57.6 3.5 %collective-permute-done.9.refs_5_ = bf16[776,256]{1,0:T(8,128)(2,1)S(1)} collective-permute-done((bf16[776,256]{1,0:T(8,128)(2,1)S(1)}, bf16[776,256]{1,0:T(8,128)(2,1)S(1)}, u32[]{:S(2)}, u32[]{:S(2)}) %collective-permute-start.9) | collective-permute-done | bytes 397344 | tf_op jit(solution)/shard_map/ppermute | solution.py:160
  61.1 5.3 %collective-permute-start.10 = (bf16[776,256]{1,0:T(8,128)(2,1)S(1)}, bf16[776,256]{1,0:T(8,128)(2,1)S(1)}, u32[]{:S(2)}, u32[]{:S(2)}) collective-permute-start(bf16[776,256]{1,0:T(8,128)(2,1)S(1)} %collective-permute-done.9.refs_5_), channel_id=1, source_target_pairs={{0,448},{64,0},{128,64},{192,128},{256,192},{320,256},{384,320},{4... | collective-permute-start | bytes 1191944 | tf_op jit(solution)/shard_map/ppermute | solution.py:160
  66.4 1.1 %collective-permute-done.2.refs_0_ = bf16[776,256]{1,0:T(8,128)(2,1)S(1)} collective-permute-done((bf16[776,256]{1,0:T(8,128)(2,1)S(1)}, bf16[776,256]{1,0:T(8,128)(2,1)S(1)}, u32[]{:S(2)}, u32[]{:S(2)}) %collective-permute-start.2) | collective-permute-done | bytes 397344 | tf_op jit(solution)/shard_map/ppermute | solution.py:160
  67.5 1.9 %collective-permute-start.3 = (bf16[776,256]{1,0:T(8,128)(2,1)S(1)}, bf16[776,256]{1,0:T(8,128)(2,1)S(1)}, u32[]{:S(2)}, u32[]{:S(2)}) collective-permute-start(bf16[776,256]{1,0:T(8,128)(2,1)S(1)} %collective-permute-done.2.refs_0_), channel_id=1, source_target_pairs={{0,64},{64,128},{128,192},{192,256},{256,320},{320,384},{384,448},... | collective-permute-start | bytes 1191944 | tf_op jit(solution)/shard_map/ppermute | solution.py:160
  69.5 2.8 %collective-permute-start.7 = (bf16[4,384,128]{2,1,0:T(8,128)(2,1)S(1)}, bf16[4,384,128]{2,1,0:T(8,128)(2,1)S(1)}, u32[]{:S(2)}, u32[]{:S(2)}) collective-permute-start(bf16[4,384,128]{2,1,0:T(8,128)(2,1)S(1)} %slice.9), channel_id=1, source_target_pairs={{0,48},{16,0},{32,16},{48,32},{1,49},{17,1},{33,17},{49,33},{2,50}... | collective-permute-start | bytes 1179656 | tf_op jit(solution)/shard_map/ppermute | solution.py:160
  72.4 2.5 %collective-permute-start.6 = (bf16[4,384,128]{2,1,0:T(8,128)(2,1)S(1)}, bf16[4,384,128]{2,1,0:T(8,128)(2,1)S(1)}, u32[]{:S(2)}, u32[]{:S(2)}) collective-permute-start(bf16[4,384,128]{2,1,0:T(8,128)(2,1)S(1)} %slice.8), channel_id=1, source_target_pairs={{0,16},{16,32},{32,48},{48,0},{1,17},{17,33},{33,49},{49,1},{2,18}... | collective-permute-start | bytes 1179656 | tf_op jit(solution)/shard_map/ppermute | solution.py:160
  74.8 5.5 %collective-permute-start.11 = (bf16[8,128]{1,0:T(8,128)(2,1)S(1)}, bf16[8,128]{1,0:T(8,128)(2,1)S(1)}, u32[]{:S(2)}, u32[]{:S(2)}) collective-permute-start(bf16[8,128]{1,0:T(8,128)(2,1)S(1)} %get-tuple-element.18), channel_id=1, source_target_pairs={{0,256},{64,320},{128,384},{192,448},{256,0},{320,64},{384,128},{4... | collective-permute-start | bytes 6152 | tf_op jit(solution)/shard_map/ppermute | solution.py:160
  80.3 2.8 %collective-permute-done.11.refs_7_ = bf16[8,128]{1,0:T(8,128)(2,1)S(1)} collective-permute-done((bf16[8,128]{1,0:T(8,128)(2,1)S(1)}, bf16[8,128]{1,0:T(8,128)(2,1)S(1)}, u32[]{:S(2)}, u32[]{:S(2)}) %collective-permute-start.11) | collective-permute-done | bytes 2080 | tf_op jit(solution)/shard_map/ppermute | solution.py:160
  83.1 1.7 %shard_map.140 = (bf16[1024,2048]{1,0:T(8,128)(2,1)}, bf16[256,2048]{1,0:T(8,128)(2,1)}, bf16[256,2048]{1,0:T(8,128)(2,1)}, bf16[8,128]{1,0:T(8,128)(2,1)S(1)}) custom-call(bf16[776,256]{1,0:T(8,128)(2,1)S(1)} %collective-permute-done.2.refs_0_, bf16[776,256]{1,0:T(8,128)(2,1)S(1)} %collective-permute-done.1.refs_1_, ...), custom_call_target="tpu_custom_call" | custom-call | flops 1048576 | bytes 1048576 | tf_op jit(solution)/shard_map/pallas_call | solution.py:146
  84.8 6.6 %collective-permute-start.12 = (bf16[8,128]{1,0:T(8,128)(2,1)S(1)}, bf16[8,128]{1,0:T(8,128)(2,1)S(1)}, u32[]{:S(2)}, u32[]{:S(2)}) collective-permute-start(bf16[8,128]{1,0:T(8,128)(2,1)S(1)} %get-tuple-element.25.mine), channel_id=1, source_target_pairs={{0,8},{8,0},{1,9},{9,1},{2,10},{10,2},{3,11},{11,3},{4,12},{12,4},... | collective-permute-start | bytes 6152 | tf_op jit(solution)/shard_map/ppermute | solution.py:222
  91.4 0.8 collective-permute-done.12.other
  92.9 1.9 %shard_map.141.refs_1_ = bf16[1024,2048]{1,0:T(8,128)(2,1)} custom-call(bf16[8,384,128]{2,1,0:T(8,128)(2,1)S(1)} %all-to-all-done.own, bf16[8,384,128]{2,1,0:T(8,128)(2,1)S(1)} %collective-permute-done.4.below, bf16[8,384,128]{2,1,0:T(8,128)(2,1)S(1)} %collective-permute-done.5.above, ...), custom_call_target="tpu_custom_call", output_to_operand_aliasing={{}: (5, {})} | custom-call | flops 1048576 | bytes 1048576 | tf_op jit(solution)/shard_map/pallas_call | solution.py:146
  (14 shorter events, 1.7 us)
Async XLA Ops:
  2.8 42.1 %all-to-all-start = ((bf16[8,384,128]{2,1,0:T(8,128)(2,1)}), bf16[8,384,128]{2,1,0:T(8,128)(2,1)S(1)}, u32[]{:S(2)}, u32[]{:S(2)}) async-start(bf16[8,384,128]{2,1,0:T(8,128)(2,1)} %get-tuple-element.17), calls=%async_computation | async-start | bytes 1572864 | tf_op jit(solution)/shard_map/all_to_all | solution.py:164
  25.4 17.5 %collective-permute-start = (bf16[776,256]{1,0:T(8,128)(2,1)S(1)}, bf16[776,256]{1,0:T(8,128)(2,1)S(1)}, u32[]{:S(2)}, u32[]{:S(2)}) collective-permute-start(bf16[776,256]{1,0:T(8,128)(2,1)S(1)} %get-tuple-element.16.refs_3_), channel_id=1, source_target_pairs={{0,64},{64,128},{128,192},{192,256},{256,320},{320,384},{384,448},... | collective-permute-start | bytes 1191944 | tf_op jit(solution)/shard_map/ppermute | solution.py:160
  28.7 21.5 %collective-permute-start.8 = (bf16[776,256]{1,0:T(8,128)(2,1)S(1)}, bf16[776,256]{1,0:T(8,128)(2,1)S(1)}, u32[]{:S(2)}, u32[]{:S(2)}) collective-permute-start(bf16[776,256]{1,0:T(8,128)(2,1)S(1)} %get-tuple-element.16.refs_3_), channel_id=1, source_target_pairs={{0,448},{64,0},{128,64},{192,128},{256,192},{320,256},{384,320},{4... | collective-permute-start | bytes 1191944 | tf_op jit(solution)/shard_map/ppermute | solution.py:160
  42.9 12.7 %collective-permute-start.1 = (bf16[776,256]{1,0:T(8,128)(2,1)S(1)}, bf16[776,256]{1,0:T(8,128)(2,1)S(1)}, u32[]{:S(2)}, u32[]{:S(2)}) collective-permute-start(bf16[776,256]{1,0:T(8,128)(2,1)S(1)} %collective-permute-done.refs_2_), channel_id=1, source_target_pairs={{0,64},{64,128},{128,192},{192,256},{256,320},{320,384},{384,448},... | collective-permute-start | bytes 1191944 | tf_op jit(solution)/shard_map/ppermute | solution.py:160
  44.9 24.6 %collective-permute-start.5 = (bf16[8,384,128]{2,1,0:T(8,128)(2,1)S(1)}, bf16[8,384,128]{2,1,0:T(8,128)(2,1)S(1)}, u32[]{:S(2)}, u32[]{:S(2)}) collective-permute-start(bf16[8,384,128]{2,1,0:T(8,128)(2,1)S(1)} %all-to-all-done.own), channel_id=1, source_target_pairs={{0,48},{16,0},{32,16},{48,32},{1,49},{17,1},{33,17},{49,33},{2,50}... | collective-permute-start | bytes 2359304 | tf_op jit(solution)/shard_map/ppermute | solution.py:160
  48.0 24.3 %collective-permute-start.4 = (bf16[8,384,128]{2,1,0:T(8,128)(2,1)S(1)}, bf16[8,384,128]{2,1,0:T(8,128)(2,1)S(1)}, u32[]{:S(2)}, u32[]{:S(2)}) collective-permute-start(bf16[8,384,128]{2,1,0:T(8,128)(2,1)S(1)} %all-to-all-done.own), channel_id=1, source_target_pairs={{0,16},{16,32},{32,48},{48,0},{1,17},{17,33},{33,49},{49,1},{2,18}... | collective-permute-start | bytes 2359304 | tf_op jit(solution)/shard_map/ppermute | solution.py:160
  50.2 10.9 %collective-permute-start.9 = (bf16[776,256]{1,0:T(8,128)(2,1)S(1)}, bf16[776,256]{1,0:T(8,128)(2,1)S(1)}, u32[]{:S(2)}, u32[]{:S(2)}) collective-permute-start(bf16[776,256]{1,0:T(8,128)(2,1)S(1)} %collective-permute-done.8.refs_4_), channel_id=1, source_target_pairs={{0,448},{64,0},{128,64},{192,128},{256,192},{320,256},{384,320},{4... | collective-permute-start | bytes 1191944 | tf_op jit(solution)/shard_map/ppermute | solution.py:160
  55.7 11.9 %collective-permute-start.2 = (bf16[776,256]{1,0:T(8,128)(2,1)S(1)}, bf16[776,256]{1,0:T(8,128)(2,1)S(1)}, u32[]{:S(2)}, u32[]{:S(2)}) collective-permute-start(bf16[776,256]{1,0:T(8,128)(2,1)S(1)} %collective-permute-done.1.refs_1_), channel_id=1, source_target_pairs={{0,64},{64,128},{128,192},{192,256},{256,320},{320,384},{384,448},... | collective-permute-start | bytes 1191944 | tf_op jit(solution)/shard_map/ppermute | solution.py:160
  61.1 22.0 %collective-permute-start.10 = (bf16[776,256]{1,0:T(8,128)(2,1)S(1)}, bf16[776,256]{1,0:T(8,128)(2,1)S(1)}, u32[]{:S(2)}, u32[]{:S(2)}) collective-permute-start(bf16[776,256]{1,0:T(8,128)(2,1)S(1)} %collective-permute-done.9.refs_5_), channel_id=1, source_target_pairs={{0,448},{64,0},{128,64},{192,128},{256,192},{320,256},{384,320},{4... | collective-permute-start | bytes 1191944 | tf_op jit(solution)/shard_map/ppermute | solution.py:160
  67.5 27.2 %collective-permute-start.3 = (bf16[776,256]{1,0:T(8,128)(2,1)S(1)}, bf16[776,256]{1,0:T(8,128)(2,1)S(1)}, u32[]{:S(2)}, u32[]{:S(2)}) collective-permute-start(bf16[776,256]{1,0:T(8,128)(2,1)S(1)} %collective-permute-done.2.refs_0_), channel_id=1, source_target_pairs={{0,64},{64,128},{128,192},{192,256},{256,320},{320,384},{384,448},... | collective-permute-start | bytes 1191944 | tf_op jit(solution)/shard_map/ppermute | solution.py:160
  69.5 23.4 %collective-permute-start.7 = (bf16[4,384,128]{2,1,0:T(8,128)(2,1)S(1)}, bf16[4,384,128]{2,1,0:T(8,128)(2,1)S(1)}, u32[]{:S(2)}, u32[]{:S(2)}) collective-permute-start(bf16[4,384,128]{2,1,0:T(8,128)(2,1)S(1)} %slice.9), channel_id=1, source_target_pairs={{0,48},{16,0},{32,16},{48,32},{1,49},{17,1},{33,17},{49,33},{2,50}... | collective-permute-start | bytes 1179656 | tf_op jit(solution)/shard_map/ppermute | solution.py:160
  72.4 20.5 %collective-permute-start.6 = (bf16[4,384,128]{2,1,0:T(8,128)(2,1)S(1)}, bf16[4,384,128]{2,1,0:T(8,128)(2,1)S(1)}, u32[]{:S(2)}, u32[]{:S(2)}) collective-permute-start(bf16[4,384,128]{2,1,0:T(8,128)(2,1)S(1)} %slice.8), channel_id=1, source_target_pairs={{0,16},{16,32},{32,48},{48,0},{1,17},{17,33},{33,49},{49,1},{2,18}... | collective-permute-start | bytes 1179656 | tf_op jit(solution)/shard_map/ppermute | solution.py:160
  74.8 8.2 %collective-permute-start.11 = (bf16[8,128]{1,0:T(8,128)(2,1)S(1)}, bf16[8,128]{1,0:T(8,128)(2,1)S(1)}, u32[]{:S(2)}, u32[]{:S(2)}) collective-permute-start(bf16[8,128]{1,0:T(8,128)(2,1)S(1)} %get-tuple-element.18), channel_id=1, source_target_pairs={{0,256},{64,320},{128,384},{192,448},{256,0},{320,64},{384,128},{4... | collective-permute-start | bytes 6152 | tf_op jit(solution)/shard_map/ppermute | solution.py:160
  84.8 7.4 %collective-permute-start.12 = (bf16[8,128]{1,0:T(8,128)(2,1)S(1)}, bf16[8,128]{1,0:T(8,128)(2,1)S(1)}, u32[]{:S(2)}, u32[]{:S(2)}) collective-permute-start(bf16[8,128]{1,0:T(8,128)(2,1)S(1)} %get-tuple-element.25.mine), channel_id=1, source_target_pairs={{0,8},{8,0},{1,9},{9,1},{2,10},{10,2},{3,11},{11,3},{4,12},{12,4},... | collective-permute-start | bytes 6152 | tf_op jit(solution)/shard_map/ppermute | solution.py:222
